TPU v7x, 128 devices: a whole 4x4x4 slice. The times are simulated.
128 devices in a mesh: fsdp: 8 (over z_hi, y), tp: 16 (over x, z_lo, core).
Axes of the slice: x: 4, y: 4, z: 4 (z_hi: 2, z_lo: 2; z = z_hi * 2 + z_lo), core: 2. Of those that a mesh axis runs over, the one named last changes fastest.
Arguments:
- merged_weight: bfloat16 [8, 8192, 10240], P(None, ('fsdp', 'tp')), may hold values from -0.0625 to 0.0625
- hidden: bfloat16 [8, 1280, 8192], P('fsdp', None, 'tp'), may hold values from -6 to 6
- group_table: int32 [16], replicated, may hold values from 0 to 15, each once
Outputs:
- query: bfloat16 [8, 1280, 8192], P('fsdp', None, 'tp')
- keyvalue: bfloat16 [8, 1280, 4096], P('fsdp', None, 'tp')
Inputs may be any that keep to these rules, and one draw needn't show every extreme that they name: `group_table`: every head group 0 .. 16 - 1 appears exactly once.
All inputs are finite; a program needn't handle non-finite values.
Results may differ from a plain program's by a relative error of at most 0.001.
Values may be sent and summed in bfloat16 or wider, within the bound.
No kernel may reach another device: no remote copies, remote signals or barrier semaphores. Data moves between devices by JAX's collectives and lax.ppermute only.
A program may use at most 128 MiB of HBM per device.

v0:
```python
import jax
import jax.numpy as jnp
import numpy as np
from jax import lax
from jax.sharding import PartitionSpec as P

Q_HEADS = 64
KV_HEADS = 8
HEAD_DIM = 128


def kv_heads_table(groups):
    per_group = max(KV_HEADS // groups, 1)
    table = np.zeros((groups, per_group), np.int32)
    for group in range(groups):
        table[group, 0] = group * per_group * KV_HEADS // (groups * per_group)
    return table


def regroup(weight, group_table, groups):
    layers, rows, _ = weight.shape
    split = Q_HEADS * HEAD_DIM
    heads = jnp.asarray(kv_heads_table(groups).reshape(-1), dtype=jnp.int32)
    q_part = weight[:, :, :split].reshape(layers, rows, groups, split // groups)
    kv_part = weight[:, :, split:].reshape(layers, rows, 2, KV_HEADS, HEAD_DIM)
    kv_part = kv_part.transpose(0, 1, 3, 2, 4)
    kv_part = jnp.take(kv_part, heads, axis=2).reshape(layers, rows, groups, -1)
    joined = jnp.concatenate([q_part, kv_part], axis=3)
    return jnp.take(joined, group_table, axis=2)


def shards(merged_weight, hidden, group_table):
    n_fsdp = lax.axis_size("fsdp")
    n_tp = lax.axis_size("tp")
    layers, rows, _ = merged_weight.shape
    local_layers, tokens_here, feat_part = hidden.shape
    grouped = regroup(merged_weight, group_table, n_tp)
    group_width = grouped.shape[3]
    sending = grouped.reshape(n_fsdp, local_layers, rows, n_tp, group_width)
    sending = sending.transpose(0, 3, 1, 2, 4).reshape(
        n_fsdp * n_tp, local_layers, rows, group_width
    )
    whole = lax.all_gather(hidden, "tp", axis=2, tiled=True)
    blocked = whole.reshape(local_layers, tokens_here, n_fsdp * n_tp, rows)
    result = jnp.einsum(
        "ltsr,slrc->ltc",
        blocked,
        lax.all_to_all(sending, ("fsdp", "tp"), split_axis=0, concat_axis=0, tiled=True),
        preferred_element_type=jnp.float32,
    )
    result = result.astype(jnp.bfloat16)
    q_width = Q_HEADS * HEAD_DIM // n_tp
    return (result[:, :, :q_width], result[:, :, q_width:])


def solution(mesh):
    return jax.shard_map(
        shards,
        mesh=mesh,
        in_specs=(P(None, ("fsdp", "tp"), None), P("fsdp", None, "tp"), P()),
        out_specs=(P("fsdp", None, "tp"), P("fsdp", None, "tp")),
        check_vma=False,
    )
```

profile of v0, /device:TPU:5, one launch (start us, length us, event | category | flops | bytes accessed | tf_op | source)
XLA Modules:
  0.0 324.8 jit_solution(11927350715356313191)
XLA Ops:
  7.2 0.0 slice-start
  7.2 0.0 all-gather.2.cloned.1.call-start
  7.2 2.6 copy.33
  9.8 0.0 all-gather.2.cloned.1.call-update
  9.8 0.0 copy-start.1
  9.8 7.6 %slice.12 = bf16[8,64,8192]{2,1,0:T(8,128)(2,1)} slice(bf16[8,64,10240]{2,1,0:T(8,128)(2,1)} %param.4), slice={[0:8], [0:64], [0:8192]} | slice | bytes 16777216 | tf_op jit(solution)/shard_map/slice | solution.py:24
  17.5 0.0 slice-done
  17.5 0.6 copy.40
  18.1 0.6 copy.50
  18.7 0.0 copy-done.1
  18.7 3.0 gather_fusion
  21.7 13.3 %copy.37 = bf16[8,64,16,2,128]{4,3,1,2,0:T(2,128)(2,1)} copy(bf16[8,64,16,2,128]{4,1,3,0,2:T(8,128)(2,1)} %bitcast.45) | data formatting | bytes 8388608 | tf_op jit(solution)/shard_map/jit(_take)/gather | solution.py:27
  35.1 0.0 copy-start.2
  35.1 7.7 %reshape.66 = bf16[8,64,16,256]{3,1,2,0:T(8,128)(2,1)} reshape(bf16[8,64,16,2,128]{4,3,1,2,0:T(2,128)(2,1)} %copy.37) | data formatting | bytes 8388608 | tf_op jit(solution)/shard_map/jit(_take)/gather | solution.py:27
  42.8 0.0 copy-start
  42.8 8.2 %copy.49 = bf16[8,8,16,8,512]{4,3,1,2,0:T(8,128)(2,1)} copy(bf16[8,8,16,8,512]{4,3,2,1,0:T(8,128)(2,1)} %bitcast.43) | data formatting | bytes 16777216 | tf_op jit(solution)/shard_map/reshape | solution.py:24
  51.0 0.0 copy-done.2
  51.0 0.0 copy-done
  51.0 10.8 %pad_maximum_fusion = bf16[8,64,16,768]{3,1,2,0:T(8,128)(2,1)} fusion(bf16[8,64,16,256]{3,1,2,0:T(8,128)(2,1)S(1)} %copy-done, bf16[8,64,16,512]{3,1,2,0:T(8,128)(2,1)} %bitcast.42), kind=kLoop, calls=%fused_computation.4 | loop fusion | flops 25165824 | bytes 25165824 | tf_op jit(solution)/shard_map/concatenate | solution.py:28
  61.8 11.4 %gather_fusion.1 = bf16[16,8,64,768]{3,2,1,0:T(8,128)(2,1)} fusion(bf16[8,64,16,768]{3,1,2,0:T(8,128)(2,1)} %pad_maximum_fusion, s32[1024]{0:T(1024)S(1)} %pad_clamp_fusion), kind=kCustom, calls=%fused_computation.1 | custom fusion | bytes 25165888 | tf_op jit(solution)/shard_map/jit(_take)/gather | solution.py:29
  73.2 6.7 %fusion.2 = bf16[8,16,1,64,768]{4,3,0,1,2:T(8,128)(2,1)S(1)} fusion(bf16[16,8,64,768]{3,2,1,0:T(8,128)(2,1)} %gather_fusion.1, pred[16]{0:T(512)(128)(4,1)S(1)} %compare_and_fusion), kind=kLoop, calls=%fused_computation.6 | loop fusion | flops 6291456 | bytes 25165840 | tf_op jit(solution)/shard_map/transpose | solution.py:40
  80.0 2.0 copy.30
  82.0 189.6 %all_to_all.5 = bf16[128,1,64,768]{3,2,1,0:T(8,128)(2,1)} all-to-all(bf16[128,1,64,768]{3,2,1,0:T(8,128)(2,1)S(1)} %bitcast.41), channel_id=1, replica_groups=mesh['fsdp'=8,'tp'=16] {'fsdp','tp'}, dimensions={0} | all-to-all | bytes 25165824 | tf_op jit(solution)/shard_map/all_to_all | solution.py:48
  271.6 16.7 %copy.32 = bf16[128,1,64,768]{0,3,2,1:T(8,128)(2,1)} copy(bf16[128,1,64,768]{3,2,1,0:T(8,128)(2,1)} %all_to_all.5) | data formatting | bytes 25165824 | tf_op jit(solution)/shard_map/all_to_all | solution.py:48
  288.3 0.0 all-gather.2.cloned.1.call-done
  288.3 27.0 %fusion.8 = bf16[1,1280,768]{1,2,0:T(8,128)(2,1)S(1)} fusion(bf16[1280,128,64]{0,2,1:T(8,128)(2,1)} %bitcast.48, bf16[128,1,64,768]{0,3,2,1:T(8,128)(2,1)} %copy.32), kind=kOutput, calls=%fused_computation.10 | convolution fusion | flops 16107110400 | bytes 35520512 | tf_op jit(solution)/shard_map/ltsr,slrc->ltc/dot_general | solution.py:45
  315.3 0.1 slice.20
  315.4 1.5 copy.35
  316.9 1.1 copy.36
  (5 shorter events, 0.1 us)
Async XLA Ops:
  7.2 10.3 %slice-start = ((bf16[8,64,10240]{2,1,0:T(8,128)(2,1)}), bf16[8,64,2048]{2,1,0:T(8,128)(2,1)S(1)}, s32[]{:S(2)}) async-start(bf16[8,64,10240]{2,1,0:T(8,128)(2,1)} %param.4), calls=%async_computation.2 | async-start | bytes 4194304 | tf_op jit(solution)/shard_map/slice | solution.py:25
  7.2 281.2 %all-gather.2.cloned.1.call-start = ((), (), s32[]{:S(2)}) async-start(), calls=%async_computation.1 | async-start | bytes 22282240 | tf_op jit(solution)/shard_map/all_gather | solution.py:43
  9.8 8.9 %copy-start.1 = (s32[16]{0:T(128)S(1)}, s32[16]{0:T(128)}, u32[]{:S(2)}) copy-start(s32[16]{0:T(128)} %constant.43) | copy-start | bytes 196
  35.1 16.0 %copy-start.2 = (s32[16]{0:T(128)S(1)}, s32[16]{0:T(128)}, u32[]{:S(2)}) copy-start(s32[16]{0:T(128)} %param.6) | copy-start | bytes 196
  42.8 8.2 %copy-start = (bf16[8,64,16,256]{3,1,2,0:T(8,128)(2,1)S(1)}, bf16[8,64,16,256]{3,1,2,0:T(8,128)(2,1)}, u32[]{:S(2)}) copy-start(bf16[8,64,16,256]{3,1,2,0:T(8,128)(2,1)} %reshape.66) | copy-start | bytes 12582916
Sparse Core Ops, SparseCore 0:
  10.3 235.7 all-gather.1
where the time goes:
time: 326 us; the launch traced here: 325 us
  blocking collectives  190 us (58%)
  local copies, waits for them, and re-layouts  76.6 us (23%)
  matrix products  27 us (8%)
  other arithmetic  17.5 us (5%)
  between operations  14.1 us (4%)
    all_to_all x1, blocking collectives, shards(): lax.all_to_all(sending, ('fsdp', 'tp'), split_axis=0, concat_axis=0, tile...  190 us
    dot_general x1, matrix products, shards(): jnp.einsum('ltsr,slrc->ltc', blocked, lax.all_to_all(sending, ('fsdp', 't...  27 us
    gather x3, local copies, waits for them, and re-layouts, regroup(): kv_part = jnp.take(kv_part, heads, axis=2).reshape(layers, rows, groups, -1)  24.1 us
    all_to_all x1, local copies, waits for them, and re-layouts, shards(): lax.all_to_all(sending, ('fsdp', 'tp'), split_axis=0, concat_axis=0, tile...  16.7 us
    gather x1, local copies, waits for them, and re-layouts, regroup(): return jnp.take(joined, group_table, axis=2)  11.4 us
    concatenate x1, other arithmetic, regroup(): joined = jnp.concatenate([q_part, kv_part], axis=3)  10.8 us
    reshape x1, local copies, waits for them, and re-layouts, regroup(): q_part = weight[:, :, :split].reshape(layers, rows, groups, split // groups)  8.23 us
    slice x1, local copies, waits for them, and re-layouts, regroup(): q_part = weight[:, :, :split].reshape(layers, rows, groups, split // groups)  7.64 us
  transfers between devices with their start and end apart: 1, of which 0 were waited for; matrix products, arithmetic and copies ran while one was open for 27% of the time, Pallas kernels for 0%

commit v1 on v0

v1 whole, which is shorter than its diff:
```python
import jax
import jax.numpy as jnp
from jax import lax
from jax.experimental import pallas as pl
from jax.experimental.pallas import tpu as pltpu
from jax.sharding import PartitionSpec as P

Q_HEADS = 64
KV_HEADS = 8
HEAD_DIM = 128


def regroup(weight, group_table):
    layers, rows, _ = weight.shape
    groups = group_table.shape[0]
    q_cols = Q_HEADS * HEAD_DIM
    q_width = q_cols // groups
    per_group = max(KV_HEADS // groups, 1)
    width = q_width + 2 * per_group * HEAD_DIM

    def body(table, src, dst, sem):
        def layer_step(layer, carry):
            for t in range(groups):
                group = table[t]
                q_at = pl.multiple_of(group * q_width, HEAD_DIM)
                pltpu.make_async_copy(
                    src.at[layer, :, pl.ds(q_at, q_width)],
                    dst.at[layer, t, :, pl.ds(0, q_width)],
                    sem,
                ).start()
                for j in range(per_group):
                    head = (group * per_group + j) * KV_HEADS // (groups * per_group)
                    for part in range(2):
                        at = pl.multiple_of(
                            q_cols + (part * KV_HEADS + head) * HEAD_DIM, HEAD_DIM
                        )
                        pltpu.make_async_copy(
                            src.at[layer, :, pl.ds(at, HEAD_DIM)],
                            dst.at[
                                layer,
                                t,
                                :,
                                pl.ds(q_width + (2 * j + part) * HEAD_DIM, HEAD_DIM),
                            ],
                            sem,
                        ).start()
            return carry

        lax.fori_loop(0, layers, layer_step, 0)
        pltpu.make_async_copy(dst, dst, sem).wait()

    return pl.pallas_call(
        body,
        out_shape=jax.ShapeDtypeStruct((layers, groups, rows, width), weight.dtype),
        in_specs=[
            pl.BlockSpec(memory_space=pltpu.SMEM),
            pl.BlockSpec(memory_space=pl.ANY),
        ],
        out_specs=pl.BlockSpec(memory_space=pl.ANY),
        scratch_shapes=[pltpu.SemaphoreType.DMA],
        name="regroup",
    )(group_table, weight)


def project(hidden, weight, q_width):
    parts, toks, feats = hidden.shape
    width = weight.shape[1]

    def body(h, w, q, kv, acc):
        k = pl.program_id(0)
        part = jnp.dot(h[0], w[...], preferred_element_type=jnp.float32)

        @pl.when(k == 0)
        def _():
            acc[...] = part

        @pl.when(k > 0)
        def _():
            acc[...] += part

        @pl.when(k == parts - 1)
        def _():
            q[...] = acc[:, :q_width].astype(q.dtype)
            kv[...] = acc[:, q_width:].astype(kv.dtype)

    return pl.pallas_call(
        body,
        grid=(parts,),
        in_specs=[
            pl.BlockSpec((1, toks, feats), lambda k: (k, 0, 0)),
            pl.BlockSpec((feats, width), lambda k: (k, 0)),
        ],
        out_specs=[
            pl.BlockSpec((toks, q_width), lambda k: (0, 0)),
            pl.BlockSpec((toks, width - q_width), lambda k: (0, 0)),
        ],
        out_shape=[
            jax.ShapeDtypeStruct((toks, q_width), hidden.dtype),
            jax.ShapeDtypeStruct((toks, width - q_width), hidden.dtype),
        ],
        scratch_shapes=[pltpu.VMEM((toks, width), jnp.float32)],
        compiler_params=pltpu.CompilerParams(vmem_limit_bytes=48 * 1024 * 1024),
        name="project",
    )(hidden, weight)


def shards(merged_weight, hidden, group_table):
    n_tp = lax.axis_size("tp")
    layers, rows, _ = merged_weight.shape
    sending = regroup(merged_weight, group_table)
    width = sending.shape[3]
    whole = lax.all_gather(hidden[0], "tp", axis=0)
    got = lax.all_to_all(
        sending.reshape(layers * n_tp, rows, width),
        ("fsdp", "tp"),
        split_axis=0,
        concat_axis=0,
        tiled=True,
    )
    q, kv = project(whole, got.reshape(-1, width), Q_HEADS * HEAD_DIM // n_tp)
    return q[None], kv[None]


def solution(mesh):
    return jax.shard_map(
        shards,
        mesh=mesh,
        in_specs=(P(None, ("fsdp", "tp"), None), P("fsdp", None, "tp"), P()),
        out_specs=(P("fsdp", None, "tp"), P("fsdp", None, "tp")),
        check_vma=False,
    )
```

time: 326 us -> 599 us (1.84); the launches traced: 325 us -> 592 us
  Pallas kernels: 0 us -> 411 us
  local copies, waits for them, and re-layouts: 76.6 us -> 0 us
  matrix products: 27 us -> 0 us
  blocking collectives: 190 us -> 166 us
  other arithmetic: 17.5 us -> 0 us
    pallas_call x0 -> x2, Pallas kernels: none -> 411 us  [the longest x1 383 us: regroup(): pl.pallas_call(body, out_shape=jax.ShapeDtypeStruct((layers, groups, rows...]
    gather x4 -> x0, local copies, waits for them, and re-layouts: 35.5 us -> none  [the longest x3 24.1 us: regroup(): kv_part = jnp.take(kv_part, heads, axis=2).reshape(layers, rows, groups, -1)]
    dot_general x1 -> x0, matrix products: 27 us -> none  [shards(): jnp.einsum('ltsr,slrc->ltc', blocked, lax.all_to_all(sending, ('fsdp', 't...]
    all_to_all x1, blocking collectives: 190 us -> 166 us  [shards(): lax.all_to_all(sending.reshape(layers * n_tp, rows, width), ('fsdp', 'tp'...]
    all_to_all x1 -> x0, local copies, waits for them, and re-layouts: 16.7 us -> none  [shards(): lax.all_to_all(sending, ('fsdp', 'tp'), split_axis=0, concat_axis=0, tile...]
    concatenate x1 -> x0, other arithmetic: 10.8 us -> none  [regroup(): joined = jnp.concatenate([q_part, kv_part], axis=3)]
    reshape x2 -> x0, local copies, waits for them, and re-layouts: 8.82 us -> none  [the longest x1 8.23 us: regroup(): q_part = weight[:, :, :split].reshape(layers, rows, groups, split // groups)]
    slice x5 -> x0, local copies, waits for them, and re-layouts: 7.78 us -> none  [the longest x1 7.64 us: regroup(): q_part = weight[:, :, :split].reshape(layers, rows, groups, split // groups)]
  transfers between devices with their start and end apart: 1 -> 1, of which waited for: 0 -> 0; matrix products, arithmetic and copies ran while one was open for 27% -> 0% of each run, Pallas kernels for 0% -> 65%
where the time goes in v1:
time: 599 us; the launch traced here: 592 us
  Pallas kernels  411 us (69%)
  blocking collectives  166 us (28%)
  between operations  14 us (2%)
    pallas_call x1, Pallas kernels, regroup(): pl.pallas_call(body, out_shape=jax.ShapeDtypeStruct((layers, groups, rows...  383 us
    all_to_all x1, blocking collectives, shards(): lax.all_to_all(sending.reshape(layers * n_tp, rows, width), ('fsdp', 'tp'...  166 us
    pallas_call x1, Pallas kernels, project(): pl.pallas_call(body, grid=(parts,), in_specs=[pl.BlockSpec((1, toks, feat...  28.2 us
  transfers between devices with their start and end apart: 1, of which 0 were waited for; matrix products, arithmetic and copies ran while one was open for 0% of the time, Pallas kernels for 65%

profile of v1, /device:TPU:5, one launch (start us, length us, event | category | flops | bytes accessed | tf_op | source)
XLA Modules:
  0.0 591.5 jit_solution(3062820189733243325)
XLA Ops:
  7.2 0.0 all-gather.2.cloned.1.call-start
  7.2 0.7 all-gather.2.cloned.1.call-update
  7.9 382.9 %regroup.1 = bf16[8,16,64,768]{3,2,1,0:T(8,128)(2,1)} custom-call(s32[16]{0:T(128)} %table.1, bf16[8,64,10240]{2,1,0:T(8,128)(2,1)} %src.1), custom_call_target="tpu_custom_call" | custom-call | tf_op jit(solution)/shard_map/regroup/pallas_call | solution.py:52
  390.9 165.6 %all_to_all.5 = bf16[128,64,768]{2,1,0:T(8,128)(2,1)} all-to-all(bf16[128,64,768]{2,1,0:T(8,128)(2,1)} %bitcast.4), channel_id=1, replica_groups=mesh['fsdp'=8,'tp'=16] {'fsdp','tp'}, dimensions={0} | all-to-all | bytes 25165824 | tf_op jit(solution)/shard_map/all_to_all | solution.py:113
  556.5 0.0 all-gather.2.cloned.1.call-done.h
  556.5 28.2 %project.1 = (bf16[1280,512]{1,0:T(8,128)(2,1)}, bf16[1280,256]{1,0:T(8,128)(2,1)}) custom-call(bf16[16,1280,512]{2,1,0:T(8,128)(2,1)} %all-gather.2.cloned.1.call-done.h, bf16[8192,768]{1,0:T(8,128)(2,1)} %bitcast.5), custom_call_target="tpu_custom_call" | custom-call | tf_op jit(solution)/shard_map/project/pallas_call | solution.py:86
Async XLA Ops:
  7.2 549.3 %all-gather.2.cloned.1.call-start = ((), (), s32[]{:S(2)}) async-start(), calls=%async_computation.1 | async-start | bytes 22282240 | tf_op jit(solution)/shard_map/all_gather | solution.py:112
Sparse Core Ops, SparseCore 0:
  9.7 421.2 all-gather.1

commit v2 on v0

v2 whole, which is shorter than its diff:
```python
import jax
import jax.numpy as jnp
import numpy as np
from jax import lax
from jax.experimental import pallas as pl
from jax.experimental.pallas import tpu as pltpu
from jax.sharding import Mesh
from jax.sharding import PartitionSpec as P


Q_HEADS = 64
KV_HEADS = 8
HEAD_DIM = 128
X = 4
Q_COLS = Q_HEADS * HEAD_DIM
NEAR = (0, 0), (0, 1), (3, 0), (1, 0)
REST = (3, 1), (1, 1), (2, 0), (2, 1)
VMEM_BYTES = 40 * 1024 * 1024


def regroup(weight, group_table):
    layers, rows, cols = weight.shape
    groups = group_table.shape[0]
    q_width = Q_COLS // groups
    width = q_width + 2 * HEAD_DIM

    def body(table, src, dst):
        for t in range(groups):
            group = table[t]
            q_at = pl.multiple_of(group * q_width, HEAD_DIM)
            dst[0, t, :, :q_width] = src[0, :, pl.ds(q_at, q_width)]
            head = group * KV_HEADS // groups
            for part in range(2):
                at = pl.multiple_of(Q_COLS + (part * KV_HEADS + head) * HEAD_DIM, HEAD_DIM)
                to = q_width + part * HEAD_DIM
                dst[0, t, :, to : to + HEAD_DIM] = src[0, :, pl.ds(at, HEAD_DIM)]

    return pl.pallas_call(
        body,
        grid_spec=pltpu.PrefetchScalarGridSpec(
            num_scalar_prefetch=1,
            grid=(layers,),
            in_specs=[pl.BlockSpec((1, rows, cols), lambda i, table: (i, 0, 0))],
            out_specs=pl.BlockSpec(
                (1, groups, rows, width), lambda i, table: (i, 0, 0, 0)
            ),
        ),
        out_shape=jax.ShapeDtypeStruct((layers, groups, rows, width), weight.dtype),
        name="regroup",
    )(group_table, weight)


def spread(hidden):
    half, quarter = hidden.shape[0] // 2, hidden.shape[0] // 4
    swap = [(0, 1), (1, 0)]

    def move(axis, pairs, value):
        return lax.ppermute(value, axis, pairs)

    def up(value):
        return move("x", [(i, (i + 1) % X) for i in range(X)], value)

    def down(value):
        return move("x", [(i, (i - 1) % X) for i in range(X)], value)

    def across(value):
        return move("zl", swap, value)

    own = hidden[:half], hidden[half:]
    z = [across(own[i]) for i in range(2)]
    left = [up(own[i]) for i in range(2)]
    right = [down(own[i]) for i in range(2)]
    left_z = up(z[0]), across(left[1])
    right_z = down(z[0]), across(right[1])
    far = up(left[0]), down(right[1])
    far_z = [up(left_z[0][:quarter]), down(right_z[0][quarter:]), across(far[1])]
    return [own, z, left, right], [left_z, right_z, far, far_z]


def both(shards):
    out = []
    for pieces in shards:
        out += [pieces, []]
        for piece in pieces:
            out[-1].append(lax.ppermute(piece, "c", [(0, 1), (1, 0)]))
    return out


def project(offsets, shards, place, weight, before, q_width, last):
    table = np.zeros((2 * X * 2, len(shards)), np.int32)
    for at in range(len(table)):
        for n in range(len(shards)):
            (dx, dz), dc = offsets[n // 2], n % 2
            x, zl, c = at // 4, at // 2 % 2, at % 2
            table[at, n] = ((x + dx) % X) * 4 + (zl ^ dz) * 2 + (c ^ dc)
    order = lax.dynamic_index_in_dim(jnp.asarray(table), place, keepdims=False)
    feats = shards[0][0].shape[1]
    toks = sum(value.shape[0] for value in shards[0])
    width = weight.shape[1]
    flat = [value for pieces in shards for value in pieces]
    steps = len(shards) // 2
    most = max(
        len(shards[2 * k]) + len(shards[2 * k + 1]) + 2 for k in range(steps)
    )

    def body(order_ref, *refs):
        pieces, refs = list(refs[: len(flat)]), refs[len(flat) :]
        w, refs = refs[0], refs[1:]
        start = None
        if before is not None:
            start, refs = refs[0], refs[1:]
        if last:
            q, kv, h_buf, w_buf, sems, total = refs
        else:
            total, h_buf, w_buf, sems = refs
        k = pl.program_id(0)

        def copies(step):
            slot, out, at = step % 2, [], 0
            for n in range(2 * step):
                at += len(shards[n])
            for n in (2 * step, 2 * step + 1):
                col = (n % 2) * feats
                row = pl.multiple_of(order_ref[n] * feats, feats)
                out.append(
                    (w.at[pl.ds(row, feats)], w_buf.at[slot, pl.ds(col, feats)])
                )
                first = 0
                for value in shards[n]:
                    to = h_buf.at[slot, pl.ds(first, value.shape[0]), pl.ds(col, feats)]
                    out.append((pieces[at], to))
                    first += value.shape[0]
                    at += 1
            return [
                pltpu.make_async_copy(a, b, sems.at[slot, i])
                for i, (a, b) in enumerate(out)
            ]

        @pl.when(k == 0)
        def _():
            for copy in copies(0):
                copy.start()

        for step in range(steps):

            @pl.when(k == step)
            def _():
                if step + 1 < steps:
                    for copy in copies(step + 1):
                        copy.start()
                for copy in copies(step):
                    copy.wait()

        @pl.when(k == 0)
        def _():
            total[...] = jnp.zeros_like(total) if before is None else start[...]

        total[...] += jnp.dot(
            h_buf[k % 2], w_buf[k % 2], preferred_element_type=jnp.float32
        )

        if last:

            @pl.when(k == steps - 1)
            def _():
                q[...] = total[:, :q_width].astype(q.dtype)
                kv[...] = total[:, q_width:].astype(kv.dtype)

    def whole(k, *_):
        return (0, 0)

    in_specs = [pl.BlockSpec(memory_space=pl.ANY)] * (len(flat) + 1)
    scratch = [
        pltpu.VMEM((2, toks, 2 * feats), jnp.bfloat16),
        pltpu.VMEM((2, 2 * feats, width), jnp.bfloat16),
        pltpu.SemaphoreType.DMA((2, most)),
    ]
    args = [order, *flat, weight]
    if before is not None:
        in_specs.append(pl.BlockSpec((toks, width), whole))
        args.append(before)
    if not last:
        out_specs = pl.BlockSpec((toks, width), whole)
        out_shape = jax.ShapeDtypeStruct((toks, width), jnp.float32)
    else:
        scratch.append(pltpu.VMEM((toks, width), jnp.float32))
        out_specs = [
            pl.BlockSpec((toks, q_width), whole),
            pl.BlockSpec((toks, width - q_width), whole),
        ]
        out_shape = [
            jax.ShapeDtypeStruct((toks, q_width), jnp.bfloat16),
            jax.ShapeDtypeStruct((toks, width - q_width), jnp.bfloat16),
        ]
    return pl.pallas_call(
        body,
        grid_spec=pltpu.PrefetchScalarGridSpec(
            num_scalar_prefetch=1,
            grid=(steps,),
            in_specs=in_specs,
            out_specs=out_specs,
            scratch_shapes=scratch,
        ),
        out_shape=out_shape,
        compiler_params=pltpu.CompilerParams(vmem_limit_bytes=VMEM_BYTES),
        name="project",
    )(*args)


def step(merged_weight, hidden, group_table):
    axes = ("zh", "y", "x", "zl", "c")
    place = lax.axis_index(("x", "zl", "c"))
    layers, rows, _ = merged_weight.shape
    groups = group_table.shape[0]
    near, rest = spread(hidden[0])
    sending = regroup(merged_weight, group_table)
    width = sending.shape[3]
    near = both(near)
    got = lax.all_to_all(
        sending.reshape(layers * groups, rows, width),
        axes,
        split_axis=0,
        concat_axis=0,
        tiled=True,
    ).reshape(-1, width)
    q_width = Q_COLS // groups
    rest = both(rest)
    sums = project(NEAR, near, place, got, None, q_width, False)
    q, kv = project(REST, rest, place, got, sums, q_width, True)
    return q[None], kv[None]


def solution(mesh):
    axes = ("zh", "y", "x", "zl", "c")
    fine = Mesh(mesh.devices.reshape(2, 4, X, 2, 2), axes)
    spec = P(("zh", "y"), None, ("x", "zl", "c"))
    return jax.shard_map(
        step,
        mesh=fine,
        in_specs=(P(None, axes, None), spec, P()),
        out_specs=(spec, spec),
        check_vma=False,
    )
```

time: 326 us -> 335 us (1.028)
  waiting for transfers between devices: 0.02 us -> 210 us
  blocking collectives: 190 us -> 0 us
  starting transfers between devices: 0.04 us -> 54.2 us
  local copies, waits for them, and re-layouts: 76.6 us -> 29.7 us
  Pallas kernels: 0 us -> 37.8 us
  matrix products: 27 us -> 0 us
  other arithmetic: 17.5 us -> 0 us
  between operations: 14.1 us -> 1.05 us
    ppermute x0 -> x32, waiting for transfers between devices: none -> 210 us  [the longest x15 209 us: move(): return lax.ppermute(value, axis, pairs)]
    all_to_all x1 -> x0, blocking collectives: 190 us -> none  [shards(): lax.all_to_all(sending, ('fsdp', 'tp'), split_axis=0, concat_axis=0, tile...]
    ppermute x0 -> x32, starting transfers between devices: none -> 43.1 us  [the longest x15 33.9 us: move(): return lax.ppermute(value, axis, pairs)]
    pallas_call x0 -> x3, Pallas kernels: none -> 37.8 us  [the longest x2 26.1 us: project(): pl.pallas_call(body, grid_spec=pltpu.PrefetchScalarGridSpec(num_scalar_pr...]
    gather x4 -> x0, local copies, waits for them, and re-layouts: 35.5 us -> none  [the longest x3 24.1 us: regroup(): kv_part = jnp.take(kv_part, heads, axis=2).reshape(layers, rows, groups, -1)]
    dot_general x1 -> x0, matrix products: 27 us -> none  [shards(): jnp.einsum('ltsr,slrc->ltc', blocked, lax.all_to_all(sending, ('fsdp', 't...]
    unnamed x10 -> x82, local copies, waits for them, and re-layouts: 5.74 us -> 28.9 us
    all_to_all x1 -> x0, local copies, waits for them, and re-layouts: 16.7 us -> none  [shards(): lax.all_to_all(sending, ('fsdp', 'tp'), split_axis=0, concat_axis=0, tile...]
  transfers between devices with their start and end apart: 1 -> 33, of which waited for: 0 -> 9; matrix products, arithmetic and copies ran while one was open for 27% -> 0% of each run, Pallas kernels for 0% -> 4%
where the time goes in v2:
time: 335 us; the launch traced here: 332 us
  waiting for transfers between devices  210 us (63%)
  starting transfers between devices  54.2 us (16%)
  Pallas kernels  37.8 us (11%)
  local copies, waits for them, and re-layouts  29.7 us (9%)
    ppermute x15, waiting for transfers between devices, move(): return lax.ppermute(value, axis, pairs)  209 us
    ppermute x15, starting transfers between devices, move(): return lax.ppermute(value, axis, pairs)  33.9 us
    unnamed x82, local copies, waits for them, and re-layouts  28.9 us
    pallas_call x2, Pallas kernels, project(): pl.pallas_call(body, grid_spec=pltpu.PrefetchScalarGridSpec(num_scalar_pr...  26.1 us
    pallas_call x1, Pallas kernels, regroup(): pl.pallas_call(body, grid_spec=pltpu.PrefetchScalarGridSpec(num_scalar_pr...  11.7 us
    all_to_all x1, starting transfers between devices, step(): lax.all_to_all(sending.reshape(layers * groups, rows, width), axes, split...  11.2 us
    ppermute x17, starting transfers between devices, both(): out[-1].append(lax.ppermute(piece, 'c', [(0, 1), (1, 0)]))  9.18 us
  transfers between devices with their start and end apart: 33, of which 9 were waited for; matrix products, arithmetic and copies ran while one was open for 0% of the time, Pallas kernels for 4%

profile of v2, /device:TPU:5, one launch (start us, length us, event | category | flops | bytes accessed | tf_op | source)
XLA Modules:
  0.0 332.4 jit_solution(3262619085922395435)
XLA Ops:
  0.6 11.7 %regroup.1 = bf16[8,16,64,768]{3,2,1,0:T(8,128)(2,1)} custom-call(s32[16]{0:T(128)} %table.1, bf16[8,64,10240]{2,1,0:T(8,128)(2,1)} %src.1), custom_call_target="tpu_custom_call" | custom-call | tf_op jit(solution)/shard_map/regroup/pallas_call | solution.py:38
  12.3 11.2 %all-to-all-start = ((bf16[128,64,768]{2,1,0:T(8,128)(2,1)}), bf16[128,64,768]{2,1,0:T(8,128)(2,1)}, u32[]{:S(2)}, u32[]{:S(2)}) async-start(bf16[128,64,768]{2,1,0:T(8,128)(2,1)} %bitcast.12), calls=%async_computation | async-start | bytes 25165824 | tf_op jit(solution)/shard_map/all_to_all | solution.py:219
  23.6 1.4 collective-permute-start
  25.3 1.2 collective-permute-start.11
  26.5 2.1 collective-permute-start.2
  28.7 142.3 %collective-permute-done.refs_4_ = bf16[640,512]{1,0:T(8,128)(2,1)S(1)} collective-permute-done((bf16[640,512]{1,0:T(8,128)(2,1)S(1)}, bf16[640,512]{1,0:T(8,128)(2,1)S(1)}, u32[]{:S(2)}, u32[]{:S(2)}) %collective-permute-start) | collective-permute-done | bytes 655392 | tf_op jit(solution)/shard_map/ppermute | solution.py:58
  171.0 30.8 %collective-permute-done.7.refs_13_ = bf16[640,512]{1,0:T(8,128)(2,1)S(1)} collective-permute-done((bf16[640,512]{1,0:T(8,128)(2,1)S(1)}, bf16[640,512]{1,0:T(8,128)(2,1)S(1)}, u32[]{:S(2)}, u32[]{:S(2)}) %collective-permute-start.7) | collective-permute-done | bytes 655392 | tf_op jit(solution)/shard_map/ppermute | solution.py:58
  201.8 1.5 collective-permute-start.22
  204.0 11.9 %collective-permute-done.29.refs_12_ = bf16[640,512]{1,0:T(8,128)(2,1)S(1)} collective-permute-done((bf16[640,512]{1,0:T(8,128)(2,1)S(1)}, bf16[640,512]{1,0:T(8,128)(2,1)S(1)}, u32[]{:S(2)}, u32[]{:S(2)}) %collective-permute-start.29) | collective-permute-done | bytes 655392 | tf_op jit(solution)/shard_map/ppermute | solution.py:58
  221.7 15.3 %collective-permute-start.6 = (bf16[640,512]{1,0:T(8,128)(2,1)S(1)}, bf16[640,512]{1,0:T(8,128)(2,1)S(1)}, u32[]{:S(2)}, u32[]{:S(2)}) collective-permute-start(bf16[640,512]{1,0:T(8,128)(2,1)S(1)} %collective-permute-done.refs_4_), channel_id=1, source_target_pairs={{0,12},{4,0},{8,4},{12,8},{1,13},{5,1},{9,5},{13,9},{2,14},{6,2},{... | collective-permute-start | bytes 1966088 | tf_op jit(solution)/shard_map/ppermute | solution.py:58
  239.8 1.7 collective-permute-start.13
  242.4 2.6 collective-permute-start.8
  245.0 6.2 %collective-permute-done.1.refs_0_ = bf16[640,512]{1,0:T(8,128)(2,1)S(1)} collective-permute-done((bf16[640,512]{1,0:T(8,128)(2,1)S(1)}, bf16[640,512]{1,0:T(8,128)(2,1)S(1)}, u32[]{:S(2)}, u32[]{:S(2)}) %collective-permute-start.1) | collective-permute-done | bytes 655392 | tf_op jit(solution)/shard_map/ppermute | solution.py:58
  251.6 2.6 collective-permute-start.3
  256.0 2.3 collective-permute-start.16
  258.3 7.4 %collective-permute-done.13.refs_9_ = bf16[640,512]{1,0:T(8,128)(2,1)S(1)} collective-permute-done((bf16[640,512]{1,0:T(8,128)(2,1)S(1)}, bf16[640,512]{1,0:T(8,128)(2,1)S(1)}, u32[]{:S(2)}, u32[]{:S(2)}) %collective-permute-start.13) | collective-permute-done | bytes 655392 | tf_op jit(solution)/shard_map/ppermute | solution.py:58
  265.7 1.6 collective-permute-start.17
  267.3 2.6 collective-permute-start.18
  269.9 1.4 collective-permute-start.15
  272.1 1.8 collective-permute-done.3.refs_1_
  274.0 1.3 collective-permute-start.4
  279.5 8.6 %collective-permute-done.18.refs_14_ = bf16[640,512]{1,0:T(8,128)(2,1)} collective-permute-done((bf16[640,512]{1,0:T(8,128)(2,1)S(1)}, bf16[640,512]{1,0:T(8,128)(2,1)}, u32[]{:S(2)}, u32[]{:S(2)}) %collective-permute-start.18) | collective-permute-done | bytes 655392 | tf_op jit(solution)/shard_map/ppermute | solution.py:58
  291.8 1.1 copy-done.1
  292.9 1.1 copy-done.3
  294.0 1.1 copy-done.5
  295.1 1.1 copy-done.7
  296.2 1.1 copy-done.9
  297.3 1.1 copy-done.11
  298.4 1.1 copy-done.13
  301.6 1.1 copy-done.19
  306.0 12.6 %project.2.refs_19_ = f32[1280,768]{1,0:T(8,128)S(1)} custom-call(s32[8]{0:T(128)S(1)} %get-tuple-element.8.order_ref, bf16[640,512]{1,0:T(8,128)(2,1)S(1)} %get-tuple-element.7.refs_0_, bf16[640,512]{1,0:T(8,128)(2,1)S(1)} %get-tuple-element.6.refs_1_, bf16[640,512]{1,0:T(8,128)(2,1)S(1)} %copy-done.11, bf16[640,512]{1,0:T(8,128)(2,1)S(1)} %copy-done.13, ...), custom_call_target="tpu_custom_call" | custom-call | tf_op jit(solution)/shard_map/project/pallas_call | solution.py:195
  318.7 13.5 %project.3 = (bf16[1280,512]{1,0:T(8,128)(2,1)}, bf16[1280,256]{1,0:T(8,128)(2,1)}) custom-call(s32[8]{0:T(128)S(1)} %get-tuple-element.9.order_ref, bf16[640,512]{1,0:T(8,128)(2,1)S(1)} %collective-permute-done.1.refs_0_, bf16[640,512]{1,0:T(8,128)(2,1)} %collective-permute-done.3.refs_1_, bf16[640,512]{1,0:T(8,128)(2,1)S(1)} %copy-done.31, ...), custom_call_target="tpu_custom_call" | custom-call | tf_op jit(solution)/shard_map/project/pallas_call | solution.py:195
  (123 shorter events, 27.0 us)
Async XLA Ops:
  12.3 279.5 %all-to-all-start = ((bf16[128,64,768]{2,1,0:T(8,128)(2,1)}), bf16[128,64,768]{2,1,0:T(8,128)(2,1)}, u32[]{:S(2)}, u32[]{:S(2)}) async-start(bf16[128,64,768]{2,1,0:T(8,128)(2,1)} %bitcast.12), calls=%async_computation | async-start | bytes 25165824 | tf_op jit(solution)/shard_map/all_to_all | solution.py:219
  23.6 147.4 %collective-permute-start = (bf16[640,512]{1,0:T(8,128)(2,1)S(1)}, bf16[640,512]{1,0:T(8,128)(2,1)S(1)}, u32[]{:S(2)}, u32[]{:S(2)}) collective-permute-start(bf16[640,512]{1,0:T(8,128)(2,1)S(1)} %get-tuple-element.7.refs_0_), channel_id=1, source_target_pairs={{0,2},{2,0},{1,3},{3,1},{4,6},{6,4},{5,7},{7,5},{8,10},{10,8},{9,1... | collective-permute-start | bytes 1966088 | tf_op jit(solution)/shard_map/ppermute | solution.py:58
  25.1 176.8 %collective-permute-start.7 = (bf16[640,512]{1,0:T(8,128)(2,1)S(1)}, bf16[640,512]{1,0:T(8,128)(2,1)S(1)}, u32[]{:S(2)}, u32[]{:S(2)}) collective-permute-start(bf16[640,512]{1,0:T(8,128)(2,1)S(1)} %get-tuple-element.6.refs_1_), channel_id=1, source_target_pairs={{0,12},{4,0},{8,4},{12,8},{1,13},{5,1},{9,5},{13,9},{2,14},{6,2},{... | collective-permute-start | bytes 1966088 | tf_op jit(solution)/shard_map/ppermute | solution.py:58
  25.3 178.1 %collective-permute-start.11 = (bf16[640,512]{1,0:T(8,128)(2,1)S(1)}, bf16[640,512]{1,0:T(8,128)(2,1)S(1)}, u32[]{:S(2)}, u32[]{:S(2)}) collective-permute-start(bf16[640,512]{1,0:T(8,128)(2,1)S(1)} %get-tuple-element.7.refs_0_), channel_id=1, source_target_pairs={{0,4},{4,8},{8,12},{12,0},{1,5},{5,9},{9,13},{13,1},{2,6},{6,10},{... | collective-permute-start | bytes 1966088 | tf_op jit(solution)/shard_map/ppermute | solution.py:58
  26.5 177.0 %collective-permute-start.2 = (bf16[640,512]{1,0:T(8,128)(2,1)S(1)}, bf16[640,512]{1,0:T(8,128)(2,1)S(1)}, u32[]{:S(2)}, u32[]{:S(2)}) collective-permute-start(bf16[640,512]{1,0:T(8,128)(2,1)S(1)} %get-tuple-element.6.refs_1_), channel_id=1, source_target_pairs={{0,4},{4,8},{8,12},{12,0},{1,5},{5,9},{9,13},{13,1},{2,6},{6,10},{... | collective-permute-start | bytes 1966088 | tf_op jit(solution)/shard_map/ppermute | solution.py:58
  28.6 175.3 %collective-permute-start.24 = (bf16[640,512]{1,0:T(8,128)(2,1)S(1)}, bf16[640,512]{1,0:T(8,128)(2,1)S(1)}, u32[]{:S(2)}, u32[]{:S(2)}) collective-permute-start(bf16[640,512]{1,0:T(8,128)(2,1)S(1)} %get-tuple-element.6.refs_1_), channel_id=1, source_target_pairs={{0,2},{2,0},{1,3},{3,1},{4,6},{6,4},{5,7},{7,5},{8,10},{10,8},{9,1... | collective-permute-start | bytes 1966088 | tf_op jit(solution)/shard_map/ppermute | solution.py:58
  171.0 44.9 %collective-permute-start.29 = (bf16[640,512]{1,0:T(8,128)(2,1)S(1)}, bf16[640,512]{1,0:T(8,128)(2,1)S(1)}, u32[]{:S(2)}, u32[]{:S(2)}) collective-permute-start(bf16[640,512]{1,0:T(8,128)(2,1)S(1)} %get-tuple-element.7.refs_0_), channel_id=1, source_target_pairs={{0,12},{4,0},{8,4},{12,8},{1,13},{5,1},{9,5},{13,9},{2,14},{6,2},{... | collective-permute-start | bytes 1966088 | tf_op jit(solution)/shard_map/ppermute | solution.py:58
  201.8 15.0 %collective-permute-start.22 = (bf16[640,512]{1,0:T(8,128)(2,1)S(1)}, bf16[640,512]{1,0:T(8,128)(2,1)S(1)}, u32[]{:S(2)}, u32[]{:S(2)}) collective-permute-start(bf16[640,512]{1,0:T(8,128)(2,1)S(1)} %get-tuple-element.7.refs_0_), channel_id=1, source_target_pairs={{0,1},{1,0},{2,3},{3,2},{4,5},{5,4},{6,7},{7,6},{8,9},{9,8},{10,11... | collective-permute-start | bytes 1966088 | tf_op jit(solution)/shard_map/ppermute | solution.py:85
  203.4 14.4 %collective-permute-start.23 = (bf16[640,512]{1,0:T(8,128)(2,1)S(1)}, bf16[640,512]{1,0:T(8,128)(2,1)S(1)}, u32[]{:S(2)}, u32[]{:S(2)}) collective-permute-start(bf16[640,512]{1,0:T(8,128)(2,1)S(1)} %get-tuple-element.6.refs_1_), channel_id=1, source_target_pairs={{0,1},{1,0},{2,3},{3,2},{4,5},{5,4},{6,7},{7,6},{8,9},{9,8},{10,11... | collective-permute-start | bytes 1966088 | tf_op jit(solution)/shard_map/ppermute | solution.py:85
  203.5 16.5 %collective-permute-start.25 = (bf16[640,512]{1,0:T(8,128)(2,1)S(1)}, bf16[640,512]{1,0:T(8,128)(2,1)S(1)}, u32[]{:S(2)}, u32[]{:S(2)}) collective-permute-start(bf16[640,512]{1,0:T(8,128)(2,1)S(1)} %collective-permute-done.refs_4_), channel_id=1, source_target_pairs={{0,1},{1,0},{2,3},{3,2},{4,5},{5,4},{6,7},{7,6},{8,9},{9,8},{10,11... | collective-permute-start | bytes 1966088 | tf_op jit(solution)/shard_map/ppermute | solution.py:85
  203.9 16.9 %collective-permute-start.31 = (bf16[640,512]{1,0:T(8,128)(2,1)S(1)}, bf16[640,512]{1,0:T(8,128)(2,1)S(1)}, u32[]{:S(2)}, u32[]{:S(2)}) collective-permute-start(bf16[640,512]{1,0:T(8,128)(2,1)S(1)} %collective-permute-done.7.refs_13_), channel_id=1, source_target_pairs={{0,1},{1,0},{2,3},{3,2},{4,5},{5,4},{6,7},{7,6},{8,9},{9,8},{10,11... | collective-permute-start | bytes 1966088 | tf_op jit(solution)/shard_map/ppermute | solution.py:85
  215.9 21.0 %collective-permute-start.27 = (bf16[640,512]{1,0:T(8,128)(2,1)S(1)}, bf16[640,512]{1,0:T(8,128)(2,1)S(1)}, u32[]{:S(2)}, u32[]{:S(2)}) collective-permute-start(bf16[640,512]{1,0:T(8,128)(2,1)S(1)} %collective-permute-done.11.refs_8_), channel_id=1, source_target_pairs={{0,1},{1,0},{2,3},{3,2},{4,5},{5,4},{6,7},{7,6},{8,9},{9,8},{10,11... | collective-permute-start | bytes 1966088 | tf_op jit(solution)/shard_map/ppermute | solution.py:85
  217.8 21.2 %collective-permute-start.28 = (bf16[640,512]{1,0:T(8,128)(2,1)S(1)}, bf16[640,512]{1,0:T(8,128)(2,1)S(1)}, u32[]{:S(2)}, u32[]{:S(2)}) collective-permute-start(bf16[640,512]{1,0:T(8,128)(2,1)S(1)} %collective-permute-done.2.refs_9_), channel_id=1, source_target_pairs={{0,1},{1,0},{2,3},{3,2},{4,5},{5,4},{6,7},{7,6},{8,9},{9,8},{10,11... | collective-permute-start | bytes 1966088 | tf_op jit(solution)/shard_map/ppermute | solution.py:85
  218.6 22.9 %collective-permute-start.26 = (bf16[640,512]{1,0:T(8,128)(2,1)S(1)}, bf16[640,512]{1,0:T(8,128)(2,1)S(1)}, u32[]{:S(2)}, u32[]{:S(2)}) collective-permute-start(bf16[640,512]{1,0:T(8,128)(2,1)S(1)} %collective-permute-done.24.refs_5_), channel_id=1, source_target_pairs={{0,1},{1,0},{2,3},{3,2},{4,5},{5,4},{6,7},{7,6},{8,9},{9,8},{10,11... | collective-permute-start | bytes 1966088 | tf_op jit(solution)/shard_map/ppermute | solution.py:85
  220.8 30.4 %collective-permute-start.1 = (bf16[640,512]{1,0:T(8,128)(2,1)S(1)}, bf16[640,512]{1,0:T(8,128)(2,1)S(1)}, u32[]{:S(2)}, u32[]{:S(2)}) collective-permute-start(bf16[640,512]{1,0:T(8,128)(2,1)S(1)} %collective-permute-done.refs_4_), channel_id=1, source_target_pairs={{0,4},{4,8},{8,12},{12,0},{1,5},{5,9},{9,13},{13,1},{2,6},{6,10},{... | collective-permute-start | bytes 1966088 | tf_op jit(solution)/shard_map/ppermute | solution.py:58
  221.7 30.0 %collective-permute-start.6 = (bf16[640,512]{1,0:T(8,128)(2,1)S(1)}, bf16[640,512]{1,0:T(8,128)(2,1)S(1)}, u32[]{:S(2)}, u32[]{:S(2)}) collective-permute-start(bf16[640,512]{1,0:T(8,128)(2,1)S(1)} %collective-permute-done.refs_4_), channel_id=1, source_target_pairs={{0,12},{4,0},{8,4},{12,8},{1,13},{5,1},{9,5},{13,9},{2,14},{6,2},{... | collective-permute-start | bytes 1966088 | tf_op jit(solution)/shard_map/ppermute | solution.py:58
  237.8 17.4 %collective-permute-start.30 = (bf16[640,512]{1,0:T(8,128)(2,1)S(1)}, bf16[640,512]{1,0:T(8,128)(2,1)S(1)}, u32[]{:S(2)}, u32[]{:S(2)}) collective-permute-start(bf16[640,512]{1,0:T(8,128)(2,1)S(1)} %collective-permute-done.29.refs_12_), channel_id=1, source_target_pairs={{0,1},{1,0},{2,3},{3,2},{4,5},{5,4},{6,7},{7,6},{8,9},{9,8},{10,11... | collective-permute-start | bytes 1966088 | tf_op jit(solution)/shard_map/ppermute | solution.py:85
  239.8 25.9 %collective-permute-start.13 = (bf16[640,512]{1,0:T(8,128)(2,1)S(1)}, bf16[640,512]{1,0:T(8,128)(2,1)S(1)}, u32[]{:S(2)}, u32[]{:S(2)}) collective-permute-start(bf16[640,512]{1,0:T(8,128)(2,1)S(1)} %collective-permute-done.7.refs_13_), channel_id=1, source_target_pairs={{0,12},{4,0},{8,4},{12,8},{1,13},{5,1},{9,5},{13,9},{2,14},{6,2},{... | collective-permute-start | bytes 1966088 | tf_op jit(solution)/shard_map/ppermute | solution.py:58
  242.4 24.9 %collective-permute-start.8 = (bf16[640,512]{1,0:T(8,128)(2,1)S(1)}, bf16[640,512]{1,0:T(8,128)(2,1)}, u32[]{:S(2)}, u32[]{:S(2)}) collective-permute-start(bf16[640,512]{1,0:T(8,128)(2,1)S(1)} %collective-permute-done.7.refs_13_), channel_id=1, source_target_pairs={{0,2},{2,0},{1,3},{3,1},{4,6},{6,4},{5,7},{7,5},{8,10},{10,8},{9,1... | collective-permute-start | bytes 1966088 | tf_op jit(solution)/shard_map/ppermute | solution.py:58
  251.2 18.7 %collective-permute-start.12 = (bf16[640,512]{1,0:T(8,128)(2,1)S(1)}, bf16[640,512]{1,0:T(8,128)(2,1)}, u32[]{:S(2)}, u32[]{:S(2)}) collective-permute-start(bf16[640,512]{1,0:T(8,128)(2,1)S(1)} %collective-permute-done.11.refs_8_), channel_id=1, source_target_pairs={{0,4},{4,8},{8,12},{12,0},{1,5},{5,9},{9,13},{13,1},{2,6},{6,10},{... | collective-permute-start | bytes 1966088 | tf_op jit(solution)/shard_map/ppermute | solution.py:58
  251.6 22.4 %collective-permute-start.3 = (bf16[640,512]{1,0:T(8,128)(2,1)S(1)}, bf16[640,512]{1,0:T(8,128)(2,1)}, u32[]{:S(2)}, u32[]{:S(2)}) collective-permute-start(bf16[640,512]{1,0:T(8,128)(2,1)S(1)} %collective-permute-done.2.refs_9_), channel_id=1, source_target_pairs={{0,2},{2,0},{1,3},{3,1},{4,6},{6,4},{5,7},{7,5},{8,10},{10,8},{9,1... | collective-permute-start | bytes 1966088 | tf_op jit(solution)/shard_map/ppermute | solution.py:58
  256.0 19.3 %collective-permute-start.16 = (bf16[320,512]{1,0:T(8,128)(2,1)S(1)}, bf16[320,512]{1,0:T(8,128)(2,1)S(1)}, u32[]{:S(2)}, u32[]{:S(2)}) collective-permute-start(bf16[320,512]{1,0:T(8,128)(2,1)S(1)} %slice.24), channel_id=1, source_target_pairs={{0,4},{4,8},{8,12},{12,0},{1,5},{5,9},{9,13},{13,1},{2,6},{6,10},{... | collective-permute-start | bytes 983048 | tf_op jit(solution)/shard_map/ppermute | solution.py:58
  265.7 10.4 %collective-permute-start.17 = (bf16[320,512]{1,0:T(8,128)(2,1)S(1)}, bf16[320,512]{1,0:T(8,128)(2,1)S(1)}, u32[]{:S(2)}, u32[]{:S(2)}) collective-permute-start(bf16[320,512]{1,0:T(8,128)(2,1)S(1)} %slice.25), channel_id=1, source_target_pairs={{0,12},{4,0},{8,4},{12,8},{1,13},{5,1},{9,5},{13,9},{2,14},{6,2},{... | collective-permute-start | bytes 983048 | tf_op jit(solution)/shard_map/ppermute | solution.py:58
  267.3 20.8 %collective-permute-start.18 = (bf16[640,512]{1,0:T(8,128)(2,1)S(1)}, bf16[640,512]{1,0:T(8,128)(2,1)}, u32[]{:S(2)}, u32[]{:S(2)}) collective-permute-start(bf16[640,512]{1,0:T(8,128)(2,1)S(1)} %collective-permute-done.13.refs_9_), channel_id=1, source_target_pairs={{0,2},{2,0},{1,3},{3,1},{4,6},{6,4},{5,7},{7,5},{8,10},{10,8},{9,1... | collective-permute-start | bytes 1966088 | tf_op jit(solution)/shard_map/ppermute | solution.py:58
  269.9 19.0 %collective-permute-start.15 = (bf16[640,512]{1,0:T(8,128)(2,1)S(1)}, bf16[640,512]{1,0:T(8,128)(2,1)S(1)}, u32[]{:S(2)}, u32[]{:S(2)}) collective-permute-start(bf16[640,512]{1,0:T(8,128)(2,1)S(1)} %collective-permute-done.13.refs_9_), channel_id=1, source_target_pairs={{0,1},{1,0},{2,3},{3,2},{4,5},{5,4},{6,7},{7,6},{8,9},{9,8},{10,11... | collective-permute-start | bytes 1966088 | tf_op jit(solution)/shard_map/ppermute | solution.py:85
  274.0 15.8 %collective-permute-start.4 = (bf16[640,512]{1,0:T(8,128)(2,1)S(1)}, bf16[640,512]{1,0:T(8,128)(2,1)S(1)}, u32[]{:S(2)}, u32[]{:S(2)}) collective-permute-start(bf16[640,512]{1,0:T(8,128)(2,1)S(1)} %collective-permute-done.1.refs_0_), channel_id=1, source_target_pairs={{0,1},{1,0},{2,3},{3,2},{4,5},{5,4},{6,7},{7,6},{8,9},{9,8},{10,11... | collective-permute-start | bytes 1966088 | tf_op jit(solution)/shard_map/ppermute | solution.py:85
  276.1 2.5 collective-permute-start.20
  278.2 40.4 %collective-permute-start.9 = (bf16[640,512]{1,0:T(8,128)(2,1)S(1)}, bf16[640,512]{1,0:T(8,128)(2,1)}, u32[]{:S(2)}, u32[]{:S(2)}) collective-permute-start(bf16[640,512]{1,0:T(8,128)(2,1)S(1)} %collective-permute-done.6.refs_4_), channel_id=1, source_target_pairs={{0,1},{1,0},{2,3},{3,2},{4,5},{5,4},{6,7},{7,6},{8,9},{9,8},{10,11... | collective-permute-start | bytes 1966088 | tf_op jit(solution)/shard_map/ppermute | solution.py:85
  279.3 39.3 %collective-permute-start.10 = (bf16[640,512]{1,0:T(8,128)(2,1)}, bf16[640,512]{1,0:T(8,128)(2,1)}, u32[]{:S(2)}, u32[]{:S(2)}) collective-permute-start(bf16[640,512]{1,0:T(8,128)(2,1)} %collective-permute-done.8.refs_5_), channel_id=1, source_target_pairs={{0,1},{1,0},{2,3},{3,2},{4,5},{5,4},{6,7},{7,6},{8,9},{9,8},{10,11... | collective-permute-start | bytes 1966088 | tf_op jit(solution)/shard_map/ppermute | solution.py:85
  288.0 30.6 %collective-permute-start.14 = (bf16[640,512]{1,0:T(8,128)(2,1)}, bf16[640,512]{1,0:T(8,128)(2,1)}, u32[]{:S(2)}, u32[]{:S(2)}) collective-permute-start(bf16[640,512]{1,0:T(8,128)(2,1)} %collective-permute-done.12.refs_8_), channel_id=1, source_target_pairs={{0,1},{1,0},{2,3},{3,2},{4,5},{5,4},{6,7},{7,6},{8,9},{9,8},{10,11... | collective-permute-start | bytes 1966088 | tf_op jit(solution)/shard_map/ppermute | solution.py:85
  289.8 28.9 %collective-permute-start.5 = (bf16[640,512]{1,0:T(8,128)(2,1)}, bf16[640,512]{1,0:T(8,128)(2,1)}, u32[]{:S(2)}, u32[]{:S(2)}) collective-permute-start(bf16[640,512]{1,0:T(8,128)(2,1)} %collective-permute-done.3.refs_1_), channel_id=1, source_target_pairs={{0,1},{1,0},{2,3},{3,2},{4,5},{5,4},{6,7},{7,6},{8,9},{9,8},{10,11... | collective-permute-start | bytes 1966088 | tf_op jit(solution)/shard_map/ppermute | solution.py:85
  290.6 28.0 %collective-permute-start.21 = (bf16[640,512]{1,0:T(8,128)(2,1)}, bf16[640,512]{1,0:T(8,128)(2,1)}, u32[]{:S(2)}, u32[]{:S(2)}) collective-permute-start(bf16[640,512]{1,0:T(8,128)(2,1)} %collective-permute-done.18.refs_14_), channel_id=1, source_target_pairs={{0,1},{1,0},{2,3},{3,2},{4,5},{5,4},{6,7},{7,6},{8,9},{9,8},{10,11... | collective-permute-start | bytes 1966088 | tf_op jit(solution)/shard_map/ppermute | solution.py:85
  (42 other events, 306.8 us)

commit v3 on v2

--- a/solution.py
+++ b/solution.py
@@ -28,12 +28,12 @@
         for t in range(groups):
             group = table[t]
             q_at = pl.multiple_of(group * q_width, HEAD_DIM)
-            dst[0, t, :, :q_width] = src[0, :, pl.ds(q_at, q_width)]
+            dst[t, 0, :, :q_width] = src[0, :, pl.ds(q_at, q_width)]
             head = group * KV_HEADS // groups
             for part in range(2):
                 at = pl.multiple_of(Q_COLS + (part * KV_HEADS + head) * HEAD_DIM, HEAD_DIM)
                 to = q_width + part * HEAD_DIM
-                dst[0, t, :, to : to + HEAD_DIM] = src[0, :, pl.ds(at, HEAD_DIM)]
+                dst[t, 0, :, to : to + HEAD_DIM] = src[0, :, pl.ds(at, HEAD_DIM)]
 
     return pl.pallas_call(
         body,
@@ -42,10 +42,10 @@
             grid=(layers,),
             in_specs=[pl.BlockSpec((1, rows, cols), lambda i, table: (i, 0, 0))],
             out_specs=pl.BlockSpec(
-                (1, groups, rows, width), lambda i, table: (i, 0, 0, 0)
+                (groups, 1, rows, width), lambda i, table: (0, i, 0, 0)
             ),
         ),
-        out_shape=jax.ShapeDtypeStruct((layers, groups, rows, width), weight.dtype),
+        out_shape=jax.ShapeDtypeStruct((groups, layers, rows, width), weight.dtype),
         name="regroup",
     )(group_table, weight)
 
@@ -96,7 +96,8 @@
     order = lax.dynamic_index_in_dim(jnp.asarray(table), place, keepdims=False)
     feats = shards[0][0].shape[1]
     toks = sum(value.shape[0] for value in shards[0])
-    width = weight.shape[1]
+    rows, width = weight.shape[2:]
+    parts = feats // rows
     flat = [value for pieces in shards for value in pieces]
     steps = len(shards) // 2
     most = max(
@@ -121,10 +122,9 @@
                 at += len(shards[n])
             for n in (2 * step, 2 * step + 1):
                 col = (n % 2) * feats
-                row = pl.multiple_of(order_ref[n] * feats, feats)
-                out.append(
-                    (w.at[pl.ds(row, feats)], w_buf.at[slot, pl.ds(col, feats)])
-                )
+                device = order_ref[n]
+                source = w.at[pl.ds(device % 2 * parts, parts), device // 2]
+                out.append((source, w_buf.at[slot, pl.ds(n % 2 * parts, parts)]))
                 first = 0
                 for value in shards[n]:
                     to = h_buf.at[slot, pl.ds(first, value.shape[0]), pl.ds(col, feats)]
@@ -156,7 +156,9 @@
             total[...] = jnp.zeros_like(total) if before is None else start[...]
 
         total[...] += jnp.dot(
-            h_buf[k % 2], w_buf[k % 2], preferred_element_type=jnp.float32
+            h_buf[k % 2],
+            w_buf[k % 2].reshape(2 * feats, width),
+            preferred_element_type=jnp.float32,
         )
 
         if last:
@@ -172,7 +174,7 @@
     in_specs = [pl.BlockSpec(memory_space=pl.ANY)] * (len(flat) + 1)
     scratch = [
         pltpu.VMEM((2, toks, 2 * feats), jnp.bfloat16),
-        pltpu.VMEM((2, 2 * feats, width), jnp.bfloat16),
+        pltpu.VMEM((2, 2 * parts, rows, width), jnp.bfloat16),
         pltpu.SemaphoreType.DMA((2, most)),
     ]
     args = [order, *flat, weight]
@@ -208,7 +210,7 @@
 
 
 def step(merged_weight, hidden, group_table):
-    axes = ("zh", "y", "x", "zl", "c")
+    axes = ("x", "zl", "c", "zh", "y")
     place = lax.axis_index(("x", "zl", "c"))
     layers, rows, _ = merged_weight.shape
     groups = group_table.shape[0]
@@ -222,11 +224,10 @@
         split_axis=0,
         concat_axis=0,
         tiled=True,
-    ).reshape(-1, width)
+    ).reshape(groups, layers, rows, width)
     q_width = Q_COLS // groups
     rest = both(rest)
-    sums = project(NEAR, near, place, got, None, q_width, False)
-    q, kv = project(REST, rest, place, got, sums, q_width, True)
+    q, kv = project(NEAR + REST, near + rest, place, got, None, q_width, True)
     return q[None], kv[None]
 
 

time: 335 us -> 326 us (0.973)
  the two profiles are of different devices: /device:TPU:5 before, /device:TPU:105 now
where the time goes in v3:
time: 326 us; the launch traced here: 325 us
  waiting for transfers between devices  210 us (64%)
  starting transfers between devices  48.2 us (15%)
  Pallas kernels  34.9 us (11%)
  local copies, waits for them, and re-layouts  30.3 us (9%)
    ppermute x15, waiting for transfers between devices, move(): return lax.ppermute(value, axis, pairs)  208 us
    unnamed x74, local copies, waits for them, and re-layouts  28.5 us
    pallas_call x1, Pallas kernels, project(): pl.pallas_call(body, grid_spec=pltpu.PrefetchScalarGridSpec(num_scalar_pr...  23.2 us
    ppermute x17, starting transfers between devices, both(): out[-1].append(lax.ppermute(piece, 'c', [(0, 1), (1, 0)]))  20.1 us
    ppermute x15, starting transfers between devices, move(): return lax.ppermute(value, axis, pairs)  17.6 us
    pallas_call x1, Pallas kernels, regroup(): pl.pallas_call(body, grid_spec=pltpu.PrefetchScalarGridSpec(num_scalar_pr...  11.7 us
    all_to_all x1, starting transfers between devices, step(): lax.all_to_all(sending.reshape(layers * groups, rows, width), axes, split...  10.5 us
  transfers between devices with their start and end apart: 33, of which 13 were waited for; matrix products, arithmetic and copies ran while one was open for 1% of the time, Pallas kernels for 0%

profile of v3, /device:TPU:105, one launch (start us, length us, event | category | flops | bytes accessed | tf_op | source)
XLA Modules:
  0.0 324.5 jit_solution(13150287357293877922)
XLA Ops:
  0.6 11.7 %regroup.1 = bf16[16,8,64,768]{3,2,1,0:T(8,128)(2,1)} custom-call(s32[16]{0:T(128)} %table.1, bf16[8,64,10240]{2,1,0:T(8,128)(2,1)} %src.1), custom_call_target="tpu_custom_call" | custom-call | tf_op jit(solution)/shard_map/regroup/pallas_call | solution.py:38
  12.3 10.5 %all-to-all-start = ((bf16[128,64,768]{2,1,0:T(8,128)(2,1)}), bf16[128,64,768]{2,1,0:T(8,128)(2,1)}, u32[]{:S(2)}, u32[]{:S(2)}) async-start(bf16[128,64,768]{2,1,0:T(8,128)(2,1)} %bitcast.10), calls=%async_computation | async-start | bytes 25165824 | tf_op jit(solution)/shard_map/all_to_all | solution.py:221
  22.9 2.5 collective-permute-start.11
  26.7 3.0 collective-permute-start.10
  29.7 163.8 %collective-permute-done.11.refs_13_ = bf16[640,512]{1,0:T(8,128)(2,1)S(1)} collective-permute-done((bf16[640,512]{1,0:T(8,128)(2,1)S(1)}, bf16[640,512]{1,0:T(8,128)(2,1)S(1)}, u32[]{:S(2)}, u32[]{:S(2)}) %collective-permute-start.11) | collective-permute-done | bytes 655392 | tf_op jit(solution)/shard_map/ppermute | solution.py:58
  193.5 3.9 %collective-permute-done.7.refs_9_ = bf16[640,512]{1,0:T(8,128)(2,1)S(1)} collective-permute-done((bf16[640,512]{1,0:T(8,128)(2,1)S(1)}, bf16[640,512]{1,0:T(8,128)(2,1)S(1)}, u32[]{:S(2)}, u32[]{:S(2)}) %collective-permute-start.7) | collective-permute-done | bytes 655392 | tf_op jit(solution)/shard_map/ppermute | solution.py:58
  197.4 1.6 collective-permute-start
  199.8 4.2 %collective-permute-start.23 = (bf16[640,512]{1,0:T(8,128)(2,1)S(1)}, bf16[640,512]{1,0:T(8,128)(2,1)S(1)}, u32[]{:S(2)}, u32[]{:S(2)}) collective-permute-start(bf16[640,512]{1,0:T(8,128)(2,1)S(1)} %collective-permute-done.11.refs_13_), channel_id=1, source_target_pairs={{0,12},{4,0},{8,4},{12,8},{1,13},{5,1},{9,5},{13,9},{2,14},{6,2},{... | collective-permute-start | bytes 1966088 | tf_op jit(solution)/shard_map/ppermute | solution.py:58
  204.0 3.5 %collective-permute-done.10.refs_12_ = bf16[640,512]{1,0:T(8,128)(2,1)S(1)} collective-permute-done((bf16[640,512]{1,0:T(8,128)(2,1)S(1)}, bf16[640,512]{1,0:T(8,128)(2,1)S(1)}, u32[]{:S(2)}, u32[]{:S(2)}) %collective-permute-start.10) | collective-permute-done | bytes 655392 | tf_op jit(solution)/shard_map/ppermute | solution.py:58
  207.5 3.9 %collective-permute-done.6.refs_8_ = bf16[640,512]{1,0:T(8,128)(2,1)S(1)} collective-permute-done((bf16[640,512]{1,0:T(8,128)(2,1)S(1)}, bf16[640,512]{1,0:T(8,128)(2,1)S(1)}, u32[]{:S(2)}, u32[]{:S(2)}) %collective-permute-start.6) | collective-permute-done | bytes 655392 | tf_op jit(solution)/shard_map/ppermute | solution.py:58
  213.3 4.1 %collective-permute-start.9 = (bf16[640,512]{1,0:T(8,128)(2,1)S(1)}, bf16[640,512]{1,0:T(8,128)(2,1)S(1)}, u32[]{:S(2)}, u32[]{:S(2)}) collective-permute-start(bf16[640,512]{1,0:T(8,128)(2,1)S(1)} %collective-permute-done.7.refs_9_), channel_id=1, source_target_pairs={{0,1},{1,0},{2,3},{3,2},{4,5},{5,4},{6,7},{7,6},{8,9},{9,8},{10,11... | collective-permute-start | bytes 1966088 | tf_op jit(solution)/shard_map/ppermute | solution.py:85
  217.3 4.2 %collective-permute-done.23.refs_25_ = bf16[640,512]{1,0:T(8,128)(2,1)S(1)} collective-permute-done((bf16[640,512]{1,0:T(8,128)(2,1)S(1)}, bf16[640,512]{1,0:T(8,128)(2,1)S(1)}, u32[]{:S(2)}, u32[]{:S(2)}) %collective-permute-start.23) | collective-permute-done | bytes 655392 | tf_op jit(solution)/shard_map/ppermute | solution.py:58
  221.5 1.2 collective-permute-start.18
  222.7 3.6 %collective-permute-done.19.refs_21_ = bf16[640,512]{1,0:T(8,128)(2,1)S(1)} collective-permute-done((bf16[640,512]{1,0:T(8,128)(2,1)S(1)}, bf16[640,512]{1,0:T(8,128)(2,1)S(1)}, u32[]{:S(2)}, u32[]{:S(2)}) %collective-permute-start.19) | collective-permute-done | bytes 655392 | tf_op jit(solution)/shard_map/ppermute | solution.py:58
  226.3 2.2 collective-permute-start.14
  229.4 4.5 %collective-permute-start.5 = (bf16[640,512]{1,0:T(8,128)(2,1)S(1)}, bf16[640,512]{1,0:T(8,128)(2,1)S(1)}, u32[]{:S(2)}, u32[]{:S(2)}) collective-permute-start(bf16[640,512]{1,0:T(8,128)(2,1)S(1)} %collective-permute-done.3.refs_5_), channel_id=1, source_target_pairs={{0,1},{1,0},{2,3},{3,2},{4,5},{5,4},{6,7},{7,6},{8,9},{9,8},{10,11... | collective-permute-start | bytes 1966088 | tf_op jit(solution)/shard_map/ppermute | solution.py:85
  233.9 6.4 %collective-permute-done.15.refs_17_ = bf16[640,512]{1,0:T(8,128)(2,1)} collective-permute-done((bf16[640,512]{1,0:T(8,128)(2,1)S(1)}, bf16[640,512]{1,0:T(8,128)(2,1)}, u32[]{:S(2)}, u32[]{:S(2)}) %collective-permute-start.15) | collective-permute-done | bytes 655392 | tf_op jit(solution)/shard_map/ppermute | solution.py:58
  240.3 2.4 collective-permute-start.12
  243.5 2.2 collective-permute-start.22
  249.9 2.0 collective-permute-start.27
  252.7 10.2 %collective-permute-done.22.refs_24_ = bf16[640,512]{1,0:T(8,128)(2,1)} collective-permute-done((bf16[640,512]{1,0:T(8,128)(2,1)S(1)}, bf16[640,512]{1,0:T(8,128)(2,1)}, u32[]{:S(2)}, u32[]{:S(2)}) %collective-permute-start.22) | collective-permute-done | bytes 655392 | tf_op jit(solution)/shard_map/ppermute | solution.py:58
  266.9 2.9 collective-permute-done.26.refs_28_
  273.2 5.4 %collective-permute-done.28.refs_30_ = bf16[640,512]{1,0:T(8,128)(2,1)} collective-permute-done((bf16[640,512]{1,0:T(8,128)(2,1)S(1)}, bf16[640,512]{1,0:T(8,128)(2,1)}, u32[]{:S(2)}, u32[]{:S(2)}) %collective-permute-start.28) | collective-permute-done | bytes 655392 | tf_op jit(solution)/shard_map/ppermute | solution.py:58
  278.6 1.6 collective-permute-start.24
  284.1 1.1 copy-done.1
  285.2 1.1 copy-done.3
  286.3 1.1 copy-done.5
  287.4 1.1 copy-done.7
  288.5 1.1 copy-done.9
  291.8 1.1 copy-done.15
  296.1 1.1 copy-done.23
  301.1 23.2 %project.1 = (bf16[1280,512]{1,0:T(8,128)(2,1)}, bf16[1280,256]{1,0:T(8,128)(2,1)}) custom-call(s32[16]{0:T(128)S(1)} %dynamic-slice_bitcast_fusion.order_ref, bf16[640,512]{1,0:T(8,128)(2,1)S(1)} %get-tuple-element.7.refs_0_, bf16[640,512]{1,0:T(8,128)(2,1)S(1)} %get-tuple-element.6.refs_1_, bf16[640,512]{1,0:T(8,128)(2,1)S(1)} %copy-done.11, ...), custom_call_target="tpu_custom_call" | custom-call | tf_op jit(solution)/shard_map/project/pallas_call | solution.py:197
  (114 shorter events, 31.2 us)
Async XLA Ops:
  12.3 271.8 %all-to-all-start = ((bf16[128,64,768]{2,1,0:T(8,128)(2,1)}), bf16[128,64,768]{2,1,0:T(8,128)(2,1)}, u32[]{:S(2)}, u32[]{:S(2)}) async-start(bf16[128,64,768]{2,1,0:T(8,128)(2,1)} %bitcast.10), calls=%async_computation | async-start | bytes 25165824 | tf_op jit(solution)/shard_map/all_to_all | solution.py:221
  22.9 170.5 %collective-permute-start.11 = (bf16[640,512]{1,0:T(8,128)(2,1)S(1)}, bf16[640,512]{1,0:T(8,128)(2,1)S(1)}, u32[]{:S(2)}, u32[]{:S(2)}) collective-permute-start(bf16[640,512]{1,0:T(8,128)(2,1)S(1)} %get-tuple-element.6.refs_1_), channel_id=1, source_target_pairs={{0,12},{4,0},{8,4},{12,8},{1,13},{5,1},{9,5},{13,9},{2,14},{6,2},{... | collective-permute-start | bytes 1966088 | tf_op jit(solution)/shard_map/ppermute | solution.py:58
  25.4 171.9 %collective-permute-start.7 = (bf16[640,512]{1,0:T(8,128)(2,1)S(1)}, bf16[640,512]{1,0:T(8,128)(2,1)S(1)}, u32[]{:S(2)}, u32[]{:S(2)}) collective-permute-start(bf16[640,512]{1,0:T(8,128)(2,1)S(1)} %get-tuple-element.6.refs_1_), channel_id=1, source_target_pairs={{0,4},{4,8},{8,12},{12,0},{1,5},{5,9},{9,13},{13,1},{2,6},{6,10},{... | collective-permute-start | bytes 1966088 | tf_op jit(solution)/shard_map/ppermute | solution.py:58
  25.4 171.9 %collective-permute-start.3 = (bf16[640,512]{1,0:T(8,128)(2,1)S(1)}, bf16[640,512]{1,0:T(8,128)(2,1)S(1)}, u32[]{:S(2)}, u32[]{:S(2)}) collective-permute-start(bf16[640,512]{1,0:T(8,128)(2,1)S(1)} %get-tuple-element.6.refs_1_), channel_id=1, source_target_pairs={{0,2},{2,0},{1,3},{3,1},{4,6},{6,4},{5,7},{7,5},{8,10},{10,8},{9,1... | collective-permute-start | bytes 1966088 | tf_op jit(solution)/shard_map/ppermute | solution.py:58
  25.8 173.2 %collective-permute-start.1 = (bf16[640,512]{1,0:T(8,128)(2,1)S(1)}, bf16[640,512]{1,0:T(8,128)(2,1)S(1)}, u32[]{:S(2)}, u32[]{:S(2)}) collective-permute-start(bf16[640,512]{1,0:T(8,128)(2,1)S(1)} %get-tuple-element.6.refs_1_), channel_id=1, source_target_pairs={{0,1},{1,0},{2,3},{3,2},{4,5},{5,4},{6,7},{7,6},{8,9},{9,8},{10,11... | collective-permute-start | bytes 1966088 | tf_op jit(solution)/shard_map/ppermute | solution.py:85
  26.7 180.8 %collective-permute-start.10 = (bf16[640,512]{1,0:T(8,128)(2,1)S(1)}, bf16[640,512]{1,0:T(8,128)(2,1)S(1)}, u32[]{:S(2)}, u32[]{:S(2)}) collective-permute-start(bf16[640,512]{1,0:T(8,128)(2,1)S(1)} %get-tuple-element.7.refs_0_), channel_id=1, source_target_pairs={{0,12},{4,0},{8,4},{12,8},{1,13},{5,1},{9,5},{13,9},{2,14},{6,2},{... | collective-permute-start | bytes 1966088 | tf_op jit(solution)/shard_map/ppermute | solution.py:58
  193.4 18.0 %collective-permute-start.6 = (bf16[640,512]{1,0:T(8,128)(2,1)S(1)}, bf16[640,512]{1,0:T(8,128)(2,1)S(1)}, u32[]{:S(2)}, u32[]{:S(2)}) collective-permute-start(bf16[640,512]{1,0:T(8,128)(2,1)S(1)} %get-tuple-element.7.refs_0_), channel_id=1, source_target_pairs={{0,4},{4,8},{8,12},{12,0},{1,5},{5,9},{9,13},{13,1},{2,6},{6,10},{... | collective-permute-start | bytes 1966088 | tf_op jit(solution)/shard_map/ppermute | solution.py:58
  197.4 15.0 %collective-permute-start.2 = (bf16[640,512]{1,0:T(8,128)(2,1)S(1)}, bf16[640,512]{1,0:T(8,128)(2,1)S(1)}, u32[]{:S(2)}, u32[]{:S(2)}) collective-permute-start(bf16[640,512]{1,0:T(8,128)(2,1)S(1)} %get-tuple-element.7.refs_0_), channel_id=1, source_target_pairs={{0,2},{2,0},{1,3},{3,1},{4,6},{6,4},{5,7},{7,5},{8,10},{10,8},{9,1... | collective-permute-start | bytes 1966088 | tf_op jit(solution)/shard_map/ppermute | solution.py:58
  197.4 15.0 %collective-permute-start = (bf16[640,512]{1,0:T(8,128)(2,1)S(1)}, bf16[640,512]{1,0:T(8,128)(2,1)S(1)}, u32[]{:S(2)}, u32[]{:S(2)}) collective-permute-start(bf16[640,512]{1,0:T(8,128)(2,1)S(1)} %get-tuple-element.7.refs_0_), channel_id=1, source_target_pairs={{0,1},{1,0},{2,3},{3,2},{4,5},{5,4},{6,7},{7,6},{8,9},{9,8},{10,11... | collective-permute-start | bytes 1966088 | tf_op jit(solution)/shard_map/ppermute | solution.py:85
  199.8 21.7 %collective-permute-start.23 = (bf16[640,512]{1,0:T(8,128)(2,1)S(1)}, bf16[640,512]{1,0:T(8,128)(2,1)S(1)}, u32[]{:S(2)}, u32[]{:S(2)}) collective-permute-start(bf16[640,512]{1,0:T(8,128)(2,1)S(1)} %collective-permute-done.11.refs_13_), channel_id=1, source_target_pairs={{0,12},{4,0},{8,4},{12,8},{1,13},{5,1},{9,5},{13,9},{2,14},{6,2},{... | collective-permute-start | bytes 1966088 | tf_op jit(solution)/shard_map/ppermute | solution.py:58
  207.5 18.8 %collective-permute-start.19 = (bf16[640,512]{1,0:T(8,128)(2,1)S(1)}, bf16[640,512]{1,0:T(8,128)(2,1)S(1)}, u32[]{:S(2)}, u32[]{:S(2)}) collective-permute-start(bf16[640,512]{1,0:T(8,128)(2,1)S(1)} %collective-permute-done.11.refs_13_), channel_id=1, source_target_pairs={{0,2},{2,0},{1,3},{3,1},{4,6},{6,4},{5,7},{7,5},{8,10},{10,8},{9,1... | collective-permute-start | bytes 1966088 | tf_op jit(solution)/shard_map/ppermute | solution.py:58
  211.4 17.1 %collective-permute-start.13 = (bf16[640,512]{1,0:T(8,128)(2,1)S(1)}, bf16[640,512]{1,0:T(8,128)(2,1)S(1)}, u32[]{:S(2)}, u32[]{:S(2)}) collective-permute-start(bf16[640,512]{1,0:T(8,128)(2,1)S(1)} %collective-permute-done.11.refs_13_), channel_id=1, source_target_pairs={{0,1},{1,0},{2,3},{3,2},{4,5},{5,4},{6,7},{7,6},{8,9},{9,8},{10,11... | collective-permute-start | bytes 1966088 | tf_op jit(solution)/shard_map/ppermute | solution.py:85
  212.4 27.9 %collective-permute-start.15 = (bf16[640,512]{1,0:T(8,128)(2,1)S(1)}, bf16[640,512]{1,0:T(8,128)(2,1)}, u32[]{:S(2)}, u32[]{:S(2)}) collective-permute-start(bf16[640,512]{1,0:T(8,128)(2,1)S(1)} %collective-permute-done.7.refs_9_), channel_id=1, source_target_pairs={{0,2},{2,0},{1,3},{3,1},{4,6},{6,4},{5,7},{7,5},{8,10},{10,8},{9,1... | collective-permute-start | bytes 1966088 | tf_op jit(solution)/shard_map/ppermute | solution.py:58
  213.3 29.5 %collective-permute-start.9 = (bf16[640,512]{1,0:T(8,128)(2,1)S(1)}, bf16[640,512]{1,0:T(8,128)(2,1)S(1)}, u32[]{:S(2)}, u32[]{:S(2)}) collective-permute-start(bf16[640,512]{1,0:T(8,128)(2,1)S(1)} %collective-permute-done.7.refs_9_), channel_id=1, source_target_pairs={{0,1},{1,0},{2,3},{3,2},{4,5},{5,4},{6,7},{7,6},{8,9},{9,8},{10,11... | collective-permute-start | bytes 1966088 | tf_op jit(solution)/shard_map/ppermute | solution.py:85
  221.5 24.2 %collective-permute-start.18 = (bf16[640,512]{1,0:T(8,128)(2,1)S(1)}, bf16[640,512]{1,0:T(8,128)(2,1)}, u32[]{:S(2)}, u32[]{:S(2)}) collective-permute-start(bf16[640,512]{1,0:T(8,128)(2,1)S(1)} %collective-permute-done.2.refs_4_), channel_id=1, source_target_pairs={{0,12},{4,0},{8,4},{12,8},{1,13},{5,1},{9,5},{13,9},{2,14},{6,2},{... | collective-permute-start | bytes 1966088 | tf_op jit(solution)/shard_map/ppermute | solution.py:58
  226.3 20.6 %collective-permute-start.14 = (bf16[640,512]{1,0:T(8,128)(2,1)S(1)}, bf16[640,512]{1,0:T(8,128)(2,1)S(1)}, u32[]{:S(2)}, u32[]{:S(2)}) collective-permute-start(bf16[640,512]{1,0:T(8,128)(2,1)S(1)} %collective-permute-done.2.refs_4_), channel_id=1, source_target_pairs={{0,4},{4,8},{8,12},{12,0},{1,5},{5,9},{9,13},{13,1},{2,6},{6,10},{... | collective-permute-start | bytes 1966088 | tf_op jit(solution)/shard_map/ppermute | solution.py:58
  229.4 19.7 %collective-permute-start.5 = (bf16[640,512]{1,0:T(8,128)(2,1)S(1)}, bf16[640,512]{1,0:T(8,128)(2,1)S(1)}, u32[]{:S(2)}, u32[]{:S(2)}) collective-permute-start(bf16[640,512]{1,0:T(8,128)(2,1)S(1)} %collective-permute-done.3.refs_5_), channel_id=1, source_target_pairs={{0,1},{1,0},{2,3},{3,2},{4,5},{5,4},{6,7},{7,6},{8,9},{9,8},{10,11... | collective-permute-start | bytes 1966088 | tf_op jit(solution)/shard_map/ppermute | solution.py:85
  240.3 11.6 %collective-permute-start.12 = (bf16[640,512]{1,0:T(8,128)(2,1)S(1)}, bf16[640,512]{1,0:T(8,128)(2,1)S(1)}, u32[]{:S(2)}, u32[]{:S(2)}) collective-permute-start(bf16[640,512]{1,0:T(8,128)(2,1)S(1)} %collective-permute-done.10.refs_12_), channel_id=1, source_target_pairs={{0,1},{1,0},{2,3},{3,2},{4,5},{5,4},{6,7},{7,6},{8,9},{9,8},{10,11... | collective-permute-start | bytes 1966088 | tf_op jit(solution)/shard_map/ppermute | solution.py:85
  243.5 19.4 %collective-permute-start.22 = (bf16[640,512]{1,0:T(8,128)(2,1)S(1)}, bf16[640,512]{1,0:T(8,128)(2,1)}, u32[]{:S(2)}, u32[]{:S(2)}) collective-permute-start(bf16[640,512]{1,0:T(8,128)(2,1)S(1)} %collective-permute-done.6.refs_8_), channel_id=1, source_target_pairs={{0,4},{4,8},{8,12},{12,0},{1,5},{5,9},{9,13},{13,1},{2,6},{6,10},{... | collective-permute-start | bytes 1966088 | tf_op jit(solution)/shard_map/ppermute | solution.py:58
  245.7 17.2 %collective-permute-start.8 = (bf16[640,512]{1,0:T(8,128)(2,1)S(1)}, bf16[640,512]{1,0:T(8,128)(2,1)S(1)}, u32[]{:S(2)}, u32[]{:S(2)}) collective-permute-start(bf16[640,512]{1,0:T(8,128)(2,1)S(1)} %collective-permute-done.6.refs_8_), channel_id=1, source_target_pairs={{0,1},{1,0},{2,3},{3,2},{4,5},{5,4},{6,7},{7,6},{8,9},{9,8},{10,11... | collective-permute-start | bytes 1966088 | tf_op jit(solution)/shard_map/ppermute | solution.py:85
  246.9 18.0 %collective-permute-start.4 = (bf16[640,512]{1,0:T(8,128)(2,1)S(1)}, bf16[640,512]{1,0:T(8,128)(2,1)S(1)}, u32[]{:S(2)}, u32[]{:S(2)}) collective-permute-start(bf16[640,512]{1,0:T(8,128)(2,1)S(1)} %collective-permute-done.2.refs_4_), channel_id=1, source_target_pairs={{0,1},{1,0},{2,3},{3,2},{4,5},{5,4},{6,7},{7,6},{8,9},{9,8},{10,11... | collective-permute-start | bytes 1966088 | tf_op jit(solution)/shard_map/ppermute | solution.py:85
  249.9 15.8 %collective-permute-start.27 = (bf16[320,512]{1,0:T(8,128)(2,1)S(1)}, bf16[320,512]{1,0:T(8,128)(2,1)S(1)}, u32[]{:S(2)}, u32[]{:S(2)}) collective-permute-start(bf16[320,512]{1,0:T(8,128)(2,1)S(1)} %slice.25), channel_id=1, source_target_pairs={{0,12},{4,0},{8,4},{12,8},{1,13},{5,1},{9,5},{13,9},{2,14},{6,2},{... | collective-permute-start | bytes 983048 | tf_op jit(solution)/shard_map/ppermute | solution.py:58
  252.7 17.1 %collective-permute-start.26 = (bf16[320,512]{1,0:T(8,128)(2,1)S(1)}, bf16[320,512]{1,0:T(8,128)(2,1)S(1)}, u32[]{:S(2)}, u32[]{:S(2)}) collective-permute-start(bf16[320,512]{1,0:T(8,128)(2,1)S(1)} %slice.24), channel_id=1, source_target_pairs={{0,4},{4,8},{8,12},{12,0},{1,5},{5,9},{9,13},{13,1},{2,6},{6,10},{... | collective-permute-start | bytes 983048 | tf_op jit(solution)/shard_map/ppermute | solution.py:58
  262.9 15.6 %collective-permute-start.28 = (bf16[640,512]{1,0:T(8,128)(2,1)S(1)}, bf16[640,512]{1,0:T(8,128)(2,1)}, u32[]{:S(2)}, u32[]{:S(2)}) collective-permute-start(bf16[640,512]{1,0:T(8,128)(2,1)S(1)} %collective-permute-done.23.refs_25_), channel_id=1, source_target_pairs={{0,2},{2,0},{1,3},{3,1},{4,6},{6,4},{5,7},{7,5},{8,10},{10,8},{9,1... | collective-permute-start | bytes 1966088 | tf_op jit(solution)/shard_map/ppermute | solution.py:58
  263.8 16.4 %collective-permute-start.25 = (bf16[640,512]{1,0:T(8,128)(2,1)S(1)}, bf16[640,512]{1,0:T(8,128)(2,1)S(1)}, u32[]{:S(2)}, u32[]{:S(2)}) collective-permute-start(bf16[640,512]{1,0:T(8,128)(2,1)S(1)} %collective-permute-done.23.refs_25_), channel_id=1, source_target_pairs={{0,1},{1,0},{2,3},{3,2},{4,5},{5,4},{6,7},{7,6},{8,9},{9,8},{10,11... | collective-permute-start | bytes 1966088 | tf_op jit(solution)/shard_map/ppermute | solution.py:85
  265.7 14.7 %collective-permute-start.21 = (bf16[640,512]{1,0:T(8,128)(2,1)S(1)}, bf16[640,512]{1,0:T(8,128)(2,1)S(1)}, u32[]{:S(2)}, u32[]{:S(2)}) collective-permute-start(bf16[640,512]{1,0:T(8,128)(2,1)S(1)} %collective-permute-done.19.refs_21_), channel_id=1, source_target_pairs={{0,1},{1,0},{2,3},{3,2},{4,5},{5,4},{6,7},{7,6},{8,9},{9,8},{10,11... | collective-permute-start | bytes 1966088 | tf_op jit(solution)/shard_map/ppermute | solution.py:85
  265.7 5.5 %collective-permute-start.30 = (bf16[320,512]{1,0:T(8,128)(2,1)S(1)}, bf16[320,512]{1,0:T(8,128)(2,1)S(1)}, u32[]{:S(2)}, u32[]{:S(2)}) collective-permute-start(bf16[320,512]{1,0:T(8,128)(2,1)S(1)} %collective-permute-done.27.refs_29_), channel_id=1, source_target_pairs={{0,1},{1,0},{2,3},{3,2},{4,5},{5,4},{6,7},{7,6},{8,9},{9,8},{10,11... | collective-permute-start | bytes 983048 | tf_op jit(solution)/shard_map/ppermute | solution.py:85
  271.9 10.3 %collective-permute-start.20 = (bf16[640,512]{1,0:T(8,128)(2,1)}, bf16[640,512]{1,0:T(8,128)(2,1)}, u32[]{:S(2)}, u32[]{:S(2)}) collective-permute-start(bf16[640,512]{1,0:T(8,128)(2,1)} %collective-permute-done.18.refs_20_), channel_id=1, source_target_pairs={{0,1},{1,0},{2,3},{3,2},{4,5},{5,4},{6,7},{7,6},{8,9},{9,8},{10,11... | collective-permute-start | bytes 1966088 | tf_op jit(solution)/shard_map/ppermute | solution.py:85
  272.7 9.3 %collective-permute-start.17 = (bf16[640,512]{1,0:T(8,128)(2,1)}, bf16[640,512]{1,0:T(8,128)(2,1)}, u32[]{:S(2)}, u32[]{:S(2)}) collective-permute-start(bf16[640,512]{1,0:T(8,128)(2,1)} %collective-permute-done.15.refs_17_), channel_id=1, source_target_pairs={{0,1},{1,0},{2,3},{3,2},{4,5},{5,4},{6,7},{7,6},{8,9},{9,8},{10,11... | collective-permute-start | bytes 1966088 | tf_op jit(solution)/shard_map/ppermute | solution.py:85
  278.6 3.7 %collective-permute-start.24 = (bf16[640,512]{1,0:T(8,128)(2,1)}, bf16[640,512]{1,0:T(8,128)(2,1)}, u32[]{:S(2)}, u32[]{:S(2)}) collective-permute-start(bf16[640,512]{1,0:T(8,128)(2,1)} %collective-permute-done.22.refs_24_), channel_id=1, source_target_pairs={{0,1},{1,0},{2,3},{3,2},{4,5},{5,4},{6,7},{7,6},{8,9},{9,8},{10,11... | collective-permute-start | bytes 1966088 | tf_op jit(solution)/shard_map/ppermute | solution.py:85
  280.2 3.0 collective-permute-start.16
  280.4 3.8 %collective-permute-start.31 = (bf16[640,512]{1,0:T(8,128)(2,1)}, bf16[640,512]{1,0:T(8,128)(2,1)}, u32[]{:S(2)}, u32[]{:S(2)}) collective-permute-start(bf16[640,512]{1,0:T(8,128)(2,1)} %collective-permute-done.28.refs_30_), channel_id=1, source_target_pairs={{0,1},{1,0},{2,3},{3,2},{4,5},{5,4},{6,7},{7,6},{8,9},{9,8},{10,11... | collective-permute-start | bytes 1966088 | tf_op jit(solution)/shard_map/ppermute | solution.py:85
  (38 other events, 311.1 us)

commit v4 on v3

--- a/solution.py
+++ b/solution.py
@@ -13,6 +13,9 @@
 HEAD_DIM = 128
 X = 4
 Q_COLS = Q_HEADS * HEAD_DIM
+AXES = ("x", "zl", "zh", "c", "y")
+SIZES = {"zh": 2, "y": 4, "x": X, "zl": 2, "c": 2}
+SPLIT = 40
 NEAR = (0, 0), (0, 1), (3, 0), (1, 0)
 REST = (3, 1), (1, 1), (2, 0), (2, 1)
 VMEM_BYTES = 40 * 1024 * 1024
@@ -26,32 +29,43 @@
 
     def body(table, src, dst):
         for t in range(groups):
+            at = {"zh": 0, "y": 0, "x": t // 4, "zl": t // 2 % 2, "c": t % 2}
+            at = tuple(at[name] for name in AXES)
             group = table[t]
             q_at = pl.multiple_of(group * q_width, HEAD_DIM)
-            dst[t, 0, :, :q_width] = src[0, :, pl.ds(q_at, q_width)]
+            dst[(*at, slice(None), slice(0, q_width))] = src[0, :, pl.ds(q_at, q_width)]
             head = group * KV_HEADS // groups
             for part in range(2):
-                at = pl.multiple_of(Q_COLS + (part * KV_HEADS + head) * HEAD_DIM, HEAD_DIM)
+                kv_at = pl.multiple_of(
+                    Q_COLS + (part * KV_HEADS + head) * HEAD_DIM, HEAD_DIM
+                )
                 to = q_width + part * HEAD_DIM
-                dst[t, 0, :, to : to + HEAD_DIM] = src[0, :, pl.ds(at, HEAD_DIM)]
-
+                dst[(*at, slice(None), slice(to, to + HEAD_DIM))] = src[
+                    0, :, pl.ds(kv_at, HEAD_DIM)
+                ]
+
+    def place(i, table):
+        at = {"zh": i // 4, "y": i % 4}
+        return (*(at.get(name, 0) for name in AXES), 0, 0)
+
+    shape = tuple(SIZES[name] for name in AXES)
+    block = tuple(1 if name in ("zh", "y") else SIZES[name] for name in AXES)
     return pl.pallas_call(
         body,
         grid_spec=pltpu.PrefetchScalarGridSpec(
             num_scalar_prefetch=1,
             grid=(layers,),
             in_specs=[pl.BlockSpec((1, rows, cols), lambda i, table: (i, 0, 0))],
-            out_specs=pl.BlockSpec(
-                (groups, 1, rows, width), lambda i, table: (0, i, 0, 0)
-            ),
+            out_specs=pl.BlockSpec((*block, rows, width), place),
         ),
-        out_shape=jax.ShapeDtypeStruct((groups, layers, rows, width), weight.dtype),
+        out_shape=jax.ShapeDtypeStruct((*shape, rows, width), weight.dtype),
         name="regroup",
     )(group_table, weight)
 
 
 def spread(hidden):
-    half, quarter = hidden.shape[0] // 2, hidden.shape[0] // 4
+    half = hidden.shape[0] * SPLIT // 80
+    quarter = half // 2
     swap = [(0, 1), (1, 0)]
 
     def move(axis, pairs, value):
@@ -86,7 +100,7 @@
     return out
 
 
-def project(offsets, shards, place, weight, before, q_width, last):
+def project(offsets, shards, place, weight, q_width):
     table = np.zeros((2 * X * 2, len(shards)), np.int32)
     for at in range(len(table)):
         for n in range(len(shards)):
@@ -96,8 +110,7 @@
     order = lax.dynamic_index_in_dim(jnp.asarray(table), place, keepdims=False)
     feats = shards[0][0].shape[1]
     toks = sum(value.shape[0] for value in shards[0])
-    rows, width = weight.shape[2:]
-    parts = feats // rows
+    rows, width = weight.shape[5:]
     flat = [value for pieces in shards for value in pieces]
     steps = len(shards) // 2
     most = max(
@@ -107,13 +120,7 @@
     def body(order_ref, *refs):
         pieces, refs = list(refs[: len(flat)]), refs[len(flat) :]
         w, refs = refs[0], refs[1:]
-        start = None
-        if before is not None:
-            start, refs = refs[0], refs[1:]
-        if last:
-            q, kv, h_buf, w_buf, sems, total = refs
-        else:
-            total, h_buf, w_buf, sems = refs
+        q, kv, h_buf, w_buf, sems, total = refs
         k = pl.program_id(0)
 
         def copies(step):
@@ -123,8 +130,10 @@
             for n in (2 * step, 2 * step + 1):
                 col = (n % 2) * feats
                 device = order_ref[n]
-                source = w.at[pl.ds(device % 2 * parts, parts), device // 2]
-                out.append((source, w_buf.at[slot, pl.ds(n % 2 * parts, parts)]))
+                pick = {"zh": device // 8, "y": device // 2 % 4}
+                pick["x"] = pl.ds(device % 2 * 2, 2)
+                source = w.at[tuple(pick.get(name, slice(None)) for name in AXES)]
+                out.append((source, w_buf.at[slot, n % 2]))
                 first = 0
                 for value in shards[n]:
                     to = h_buf.at[slot, pl.ds(first, value.shape[0]), pl.ds(col, feats)]
@@ -151,22 +160,26 @@
                 for copy in copies(step):
                     copy.wait()
 
+        def product():
+            return jnp.dot(
+                h_buf[k % 2],
+                w_buf[k % 2].reshape(2 * feats, width),
+                preferred_element_type=jnp.float32,
+            )
+
         @pl.when(k == 0)
         def _():
-            total[...] = jnp.zeros_like(total) if before is None else start[...]
-
-        total[...] += jnp.dot(
-            h_buf[k % 2],
-            w_buf[k % 2].reshape(2 * feats, width),
-            preferred_element_type=jnp.float32,
-        )
-
-        if last:
-
-            @pl.when(k == steps - 1)
-            def _():
-                q[...] = total[:, :q_width].astype(q.dtype)
-                kv[...] = total[:, q_width:].astype(kv.dtype)
+            total[...] = product()
+
+        @pl.when((k > 0) & (k < steps - 1))
+        def _():
+            total[...] += product()
+
+        @pl.when(k == steps - 1)
+        def _():
+            done = total[...] + product()
+            q[...] = done[:, :q_width].astype(q.dtype)
+            kv[...] = done[:, q_width:].astype(kv.dtype)
 
     def whole(k, *_):
         return (0, 0)
@@ -174,26 +187,19 @@
     in_specs = [pl.BlockSpec(memory_space=pl.ANY)] * (len(flat) + 1)
     scratch = [
         pltpu.VMEM((2, toks, 2 * feats), jnp.bfloat16),
-        pltpu.VMEM((2, 2 * parts, rows, width), jnp.bfloat16),
+        pltpu.VMEM((2, 2, 2, 2, 2, rows, width), jnp.bfloat16),
         pltpu.SemaphoreType.DMA((2, most)),
+        pltpu.VMEM((toks, width), jnp.float32),
     ]
     args = [order, *flat, weight]
-    if before is not None:
-        in_specs.append(pl.BlockSpec((toks, width), whole))
-        args.append(before)
-    if not last:
-        out_specs = pl.BlockSpec((toks, width), whole)
-        out_shape = jax.ShapeDtypeStruct((toks, width), jnp.float32)
-    else:
-        scratch.append(pltpu.VMEM((toks, width), jnp.float32))
-        out_specs = [
-            pl.BlockSpec((toks, q_width), whole),
-            pl.BlockSpec((toks, width - q_width), whole),
-        ]
-        out_shape = [
-            jax.ShapeDtypeStruct((toks, q_width), jnp.bfloat16),
-            jax.ShapeDtypeStruct((toks, width - q_width), jnp.bfloat16),
-        ]
+    out_specs = [
+        pl.BlockSpec((toks, q_width), whole),
+        pl.BlockSpec((toks, width - q_width), whole),
+    ]
+    out_shape = [
+        jax.ShapeDtypeStruct((toks, q_width), jnp.bfloat16),
+        jax.ShapeDtypeStruct((toks, width - q_width), jnp.bfloat16),
+    ]
     return pl.pallas_call(
         body,
         grid_spec=pltpu.PrefetchScalarGridSpec(
@@ -210,24 +216,20 @@
 
 
 def step(merged_weight, hidden, group_table):
-    axes = ("x", "zl", "c", "zh", "y")
     place = lax.axis_index(("x", "zl", "c"))
-    layers, rows, _ = merged_weight.shape
-    groups = group_table.shape[0]
     near, rest = spread(hidden[0])
     sending = regroup(merged_weight, group_table)
-    width = sending.shape[3]
     near = both(near)
     got = lax.all_to_all(
-        sending.reshape(layers * groups, rows, width),
-        axes,
+        sending.reshape(-1, *sending.shape[5:]),
+        AXES,
         split_axis=0,
         concat_axis=0,
         tiled=True,
-    ).reshape(groups, layers, rows, width)
-    q_width = Q_COLS // groups
+    ).reshape(sending.shape)
+    q_width = Q_COLS // group_table.shape[0]
     rest = both(rest)
-    q, kv = project(NEAR + REST, near + rest, place, got, None, q_width, True)
+    q, kv = project(NEAR + REST, near + rest, place, got, q_width)
     return q[None], kv[None]
 
 

time: 326 us -> 322 us (0.988)
  the two profiles are of different devices: /device:TPU:105 before, /device:TPU:5 now
where the time goes in v4:
time: 322 us; the launch traced here: 319 us
  waiting for transfers between devices  193 us (60%)
  starting transfers between devices  59.9 us (19%)
  Pallas kernels  34.3 us (11%)
  local copies, waits for them, and re-layouts  30.3 us (9%)
    ppermute x15, waiting for transfers between devices, move(): return lax.ppermute(value, axis, pairs)  191 us
    unnamed x74, local copies, waits for them, and re-layouts  28.5 us
    ppermute x15, starting transfers between devices, move(): return lax.ppermute(value, axis, pairs)  27 us
    pallas_call x1, Pallas kernels, project(): pl.pallas_call(body, grid_spec=pltpu.PrefetchScalarGridSpec(num_scalar_pr...  22.6 us
    ppermute x17, starting transfers between devices, both(): out[-1].append(lax.ppermute(piece, 'c', [(0, 1), (1, 0)]))  21.7 us
    pallas_call x1, Pallas kernels, regroup(): pl.pallas_call(body, grid_spec=pltpu.PrefetchScalarGridSpec(num_scalar_pr...  11.7 us
    all_to_all x1, starting transfers between devices, step(): lax.all_to_all(sending.reshape(-1, *sending.shape[5:]), AXES, split_axis=...  11.2 us
  transfers between devices with their start and end apart: 33, of which 12 were waited for; matrix products, arithmetic and copies ran while one was open for 1% of the time, Pallas kernels for 0%

profile of v4, /device:TPU:5, one launch (start us, length us, event | category | flops | bytes accessed | tf_op | source)
XLA Modules:
  0.0 318.8 jit_solution(6883696306051227814)
XLA Ops:
  0.6 11.7 %regroup.1 = bf16[4,2,2,2,4,64,768]{6,5,4,3,2,1,0:T(8,128)(2,1)} custom-call(s32[16]{0:T(128)} %table.1, bf16[8,64,10240]{2,1,0:T(8,128)(2,1)} %src.1), custom_call_target="tpu_custom_call" | custom-call | tf_op jit(solution)/shard_map/regroup/pallas_call | solution.py:53
  12.3 11.2 %all-to-all-start = ((bf16[128,64,768]{2,1,0:T(8,128)(2,1)}), bf16[128,64,768]{2,1,0:T(8,128)(2,1)}, u32[]{:S(2)}, u32[]{:S(2)}) async-start(bf16[128,64,768]{2,1,0:T(8,128)(2,1)} %bitcast.10), calls=%async_computation | async-start | bytes 25165824 | tf_op jit(solution)/shard_map/all_to_all | solution.py:223
  24.0 1.2 collective-permute-start.7
  25.2 1.3 collective-permute-start.3
  26.5 1.2 collective-permute-start.1
  28.0 159.3 %collective-permute-done.11.refs_13_ = bf16[640,512]{1,0:T(8,128)(2,1)S(1)} collective-permute-done((bf16[640,512]{1,0:T(8,128)(2,1)S(1)}, bf16[640,512]{1,0:T(8,128)(2,1)S(1)}, u32[]{:S(2)}, u32[]{:S(2)}) %collective-permute-start.11) | collective-permute-done | bytes 655392 | tf_op jit(solution)/shard_map/ppermute | solution.py:72
  187.3 3.5 %collective-permute-done.7.refs_9_ = bf16[640,512]{1,0:T(8,128)(2,1)S(1)} collective-permute-done((bf16[640,512]{1,0:T(8,128)(2,1)S(1)}, bf16[640,512]{1,0:T(8,128)(2,1)S(1)}, u32[]{:S(2)}, u32[]{:S(2)}) %collective-permute-start.7) | collective-permute-done | bytes 655392 | tf_op jit(solution)/shard_map/ppermute | solution.py:72
  190.9 1.1 collective-permute-start.2
  191.9 1.8 collective-permute-start
  194.6 6.0 %collective-permute-start.23 = (bf16[640,512]{1,0:T(8,128)(2,1)S(1)}, bf16[640,512]{1,0:T(8,128)(2,1)S(1)}, u32[]{:S(2)}, u32[]{:S(2)}) collective-permute-start(bf16[640,512]{1,0:T(8,128)(2,1)S(1)} %collective-permute-done.11.refs_13_), channel_id=1, source_target_pairs={{0,12},{4,0},{8,4},{12,8},{1,13},{5,1},{9,5},{13,9},{2,14},{6,2},{... | collective-permute-start | bytes 1966088 | tf_op jit(solution)/shard_map/ppermute | solution.py:72
  201.4 1.5 collective-permute-start.19
  202.9 2.9 collective-permute-done.6.refs_8_
  205.8 2.1 collective-permute-start.13
  208.8 3.4 %collective-permute-start.9 = (bf16[640,512]{1,0:T(8,128)(2,1)S(1)}, bf16[640,512]{1,0:T(8,128)(2,1)S(1)}, u32[]{:S(2)}, u32[]{:S(2)}) collective-permute-start(bf16[640,512]{1,0:T(8,128)(2,1)S(1)} %collective-permute-done.7.refs_9_), channel_id=1, source_target_pairs={{0,1},{1,0},{2,3},{3,2},{4,5},{5,4},{6,7},{7,6},{8,9},{9,8},{10,11... | collective-permute-start | bytes 1966088 | tf_op jit(solution)/shard_map/ppermute | solution.py:99
  212.2 3.2 %collective-permute-done.23.refs_25_ = bf16[640,512]{1,0:T(8,128)(2,1)S(1)} collective-permute-done((bf16[640,512]{1,0:T(8,128)(2,1)S(1)}, bf16[640,512]{1,0:T(8,128)(2,1)S(1)}, u32[]{:S(2)}, u32[]{:S(2)}) %collective-permute-start.23) | collective-permute-done | bytes 655392 | tf_op jit(solution)/shard_map/ppermute | solution.py:72
  215.4 4.9 %collective-permute-start.18 = (bf16[640,512]{1,0:T(8,128)(2,1)S(1)}, bf16[640,512]{1,0:T(8,128)(2,1)}, u32[]{:S(2)}, u32[]{:S(2)}) collective-permute-start(bf16[640,512]{1,0:T(8,128)(2,1)S(1)} %collective-permute-done.2.refs_4_), channel_id=1, source_target_pairs={{0,12},{4,0},{8,4},{12,8},{1,13},{5,1},{9,5},{13,9},{2,14},{6,2},{... | collective-permute-start | bytes 1966088 | tf_op jit(solution)/shard_map/ppermute | solution.py:72
  220.3 3.2 %collective-permute-start.14 = (bf16[640,512]{1,0:T(8,128)(2,1)S(1)}, bf16[640,512]{1,0:T(8,128)(2,1)S(1)}, u32[]{:S(2)}, u32[]{:S(2)}) collective-permute-start(bf16[640,512]{1,0:T(8,128)(2,1)S(1)} %collective-permute-done.2.refs_4_), channel_id=1, source_target_pairs={{0,4},{4,8},{8,12},{12,0},{1,5},{5,9},{9,13},{13,1},{2,6},{6,10},{... | collective-permute-start | bytes 1966088 | tf_op jit(solution)/shard_map/ppermute | solution.py:72
  224.4 5.2 %collective-permute-start.5 = (bf16[640,512]{1,0:T(8,128)(2,1)S(1)}, bf16[640,512]{1,0:T(8,128)(2,1)S(1)}, u32[]{:S(2)}, u32[]{:S(2)}) collective-permute-start(bf16[640,512]{1,0:T(8,128)(2,1)S(1)} %collective-permute-done.3.refs_5_), channel_id=1, source_target_pairs={{0,1},{1,0},{2,3},{3,2},{4,5},{5,4},{6,7},{7,6},{8,9},{9,8},{10,11... | collective-permute-start | bytes 1966088 | tf_op jit(solution)/shard_map/ppermute | solution.py:99
  229.7 4.1 %collective-permute-done.15.refs_17_ = bf16[640,512]{1,0:T(8,128)(2,1)} collective-permute-done((bf16[640,512]{1,0:T(8,128)(2,1)S(1)}, bf16[640,512]{1,0:T(8,128)(2,1)}, u32[]{:S(2)}, u32[]{:S(2)}) %collective-permute-start.15) | collective-permute-done | bytes 655392 | tf_op jit(solution)/shard_map/ppermute | solution.py:72
  233.8 2.4 collective-permute-start.12
  237.0 4.2 %collective-permute-start.22 = (bf16[640,512]{1,0:T(8,128)(2,1)S(1)}, bf16[640,512]{1,0:T(8,128)(2,1)}, u32[]{:S(2)}, u32[]{:S(2)}) collective-permute-start(bf16[640,512]{1,0:T(8,128)(2,1)S(1)} %collective-permute-done.6.refs_8_), channel_id=1, source_target_pairs={{0,4},{4,8},{8,12},{12,0},{1,5},{5,9},{9,13},{13,1},{2,6},{6,10},{... | collective-permute-start | bytes 1966088 | tf_op jit(solution)/shard_map/ppermute | solution.py:72
  245.3 1.4 collective-permute-start.27
  247.7 10.2 %collective-permute-done.22.refs_24_ = bf16[640,512]{1,0:T(8,128)(2,1)} collective-permute-done((bf16[640,512]{1,0:T(8,128)(2,1)S(1)}, bf16[640,512]{1,0:T(8,128)(2,1)}, u32[]{:S(2)}, u32[]{:S(2)}) %collective-permute-start.22) | collective-permute-done | bytes 655392 | tf_op jit(solution)/shard_map/ppermute | solution.py:72
  257.9 1.5 collective-permute-start.28
  263.3 1.6 collective-permute-done.26.refs_28_
  268.1 5.4 %collective-permute-done.28.refs_30_ = bf16[640,512]{1,0:T(8,128)(2,1)} collective-permute-done((bf16[640,512]{1,0:T(8,128)(2,1)S(1)}, bf16[640,512]{1,0:T(8,128)(2,1)}, u32[]{:S(2)}, u32[]{:S(2)}) %collective-permute-start.28) | collective-permute-done | bytes 655392 | tf_op jit(solution)/shard_map/ppermute | solution.py:72
  273.5 1.6 collective-permute-start.24
  279.1 1.1 copy-done.1
  280.2 1.1 copy-done.3
  284.5 1.1 copy-done.11
  288.9 1.1 copy-done.19
  296.0 22.6 %project.1 = (bf16[1280,512]{1,0:T(8,128)(2,1)}, bf16[1280,256]{1,0:T(8,128)(2,1)}) custom-call(s32[16]{0:T(128)S(1)} %dynamic-slice_bitcast_fusion.order_ref, bf16[640,512]{1,0:T(8,128)(2,1)S(1)} %get-tuple-element.7.refs_0_, bf16[640,512]{1,0:T(8,128)(2,1)S(1)} %get-tuple-element.6.refs_1_, bf16[640,512]{1,0:T(8,128)(2,1)S(1)} %copy-done.11, ...), custom_call_target="tpu_custom_call" | custom-call | tf_op jit(solution)/shard_map/project/pallas_call | solution.py:203
  (114 shorter events, 33.4 us)
Async XLA Ops:
  12.3 266.7 %all-to-all-start = ((bf16[128,64,768]{2,1,0:T(8,128)(2,1)}), bf16[128,64,768]{2,1,0:T(8,128)(2,1)}, u32[]{:S(2)}, u32[]{:S(2)}) async-start(bf16[128,64,768]{2,1,0:T(8,128)(2,1)} %bitcast.10), calls=%async_computation | async-start | bytes 25165824 | tf_op jit(solution)/shard_map/all_to_all | solution.py:223
  23.6 163.7 %collective-permute-start.11 = (bf16[640,512]{1,0:T(8,128)(2,1)S(1)}, bf16[640,512]{1,0:T(8,128)(2,1)S(1)}, u32[]{:S(2)}, u32[]{:S(2)}) collective-permute-start(bf16[640,512]{1,0:T(8,128)(2,1)S(1)} %get-tuple-element.6.refs_1_), channel_id=1, source_target_pairs={{0,12},{4,0},{8,4},{12,8},{1,13},{5,1},{9,5},{13,9},{2,14},{6,2},{... | collective-permute-start | bytes 1966088 | tf_op jit(solution)/shard_map/ppermute | solution.py:72
  24.0 166.9 %collective-permute-start.7 = (bf16[640,512]{1,0:T(8,128)(2,1)S(1)}, bf16[640,512]{1,0:T(8,128)(2,1)S(1)}, u32[]{:S(2)}, u32[]{:S(2)}) collective-permute-start(bf16[640,512]{1,0:T(8,128)(2,1)S(1)} %get-tuple-element.6.refs_1_), channel_id=1, source_target_pairs={{0,4},{4,8},{8,12},{12,0},{1,5},{5,9},{9,13},{13,1},{2,6},{6,10},{... | collective-permute-start | bytes 1966088 | tf_op jit(solution)/shard_map/ppermute | solution.py:72
  25.2 166.8 %collective-permute-start.3 = (bf16[640,512]{1,0:T(8,128)(2,1)S(1)}, bf16[640,512]{1,0:T(8,128)(2,1)S(1)}, u32[]{:S(2)}, u32[]{:S(2)}) collective-permute-start(bf16[640,512]{1,0:T(8,128)(2,1)S(1)} %get-tuple-element.6.refs_1_), channel_id=1, source_target_pairs={{0,2},{2,0},{1,3},{3,1},{4,6},{6,4},{5,7},{7,5},{8,10},{10,8},{9,1... | collective-permute-start | bytes 1966088 | tf_op jit(solution)/shard_map/ppermute | solution.py:72
  26.5 167.2 %collective-permute-start.1 = (bf16[640,512]{1,0:T(8,128)(2,1)S(1)}, bf16[640,512]{1,0:T(8,128)(2,1)S(1)}, u32[]{:S(2)}, u32[]{:S(2)}) collective-permute-start(bf16[640,512]{1,0:T(8,128)(2,1)S(1)} %get-tuple-element.6.refs_1_), channel_id=1, source_target_pairs={{0,1},{1,0},{2,3},{3,2},{4,5},{5,4},{6,7},{7,6},{8,9},{9,8},{10,11... | collective-permute-start | bytes 1966088 | tf_op jit(solution)/shard_map/ppermute | solution.py:99
  27.7 173.6 %collective-permute-start.10 = (bf16[640,512]{1,0:T(8,128)(2,1)S(1)}, bf16[640,512]{1,0:T(8,128)(2,1)S(1)}, u32[]{:S(2)}, u32[]{:S(2)}) collective-permute-start(bf16[640,512]{1,0:T(8,128)(2,1)S(1)} %get-tuple-element.7.refs_0_), channel_id=1, source_target_pairs={{0,12},{4,0},{8,4},{12,8},{1,13},{5,1},{9,5},{13,9},{2,14},{6,2},{... | collective-permute-start | bytes 1966088 | tf_op jit(solution)/shard_map/ppermute | solution.py:72
  187.3 18.5 %collective-permute-start.6 = (bf16[640,512]{1,0:T(8,128)(2,1)S(1)}, bf16[640,512]{1,0:T(8,128)(2,1)S(1)}, u32[]{:S(2)}, u32[]{:S(2)}) collective-permute-start(bf16[640,512]{1,0:T(8,128)(2,1)S(1)} %get-tuple-element.7.refs_0_), channel_id=1, source_target_pairs={{0,4},{4,8},{8,12},{12,0},{1,5},{5,9},{9,13},{13,1},{2,6},{6,10},{... | collective-permute-start | bytes 1966088 | tf_op jit(solution)/shard_map/ppermute | solution.py:72
  190.9 17.1 %collective-permute-start.2 = (bf16[640,512]{1,0:T(8,128)(2,1)S(1)}, bf16[640,512]{1,0:T(8,128)(2,1)S(1)}, u32[]{:S(2)}, u32[]{:S(2)}) collective-permute-start(bf16[640,512]{1,0:T(8,128)(2,1)S(1)} %get-tuple-element.7.refs_0_), channel_id=1, source_target_pairs={{0,2},{2,0},{1,3},{3,1},{4,6},{6,4},{5,7},{7,5},{8,10},{10,8},{9,1... | collective-permute-start | bytes 1966088 | tf_op jit(solution)/shard_map/ppermute | solution.py:72
  191.9 16.0 %collective-permute-start = (bf16[640,512]{1,0:T(8,128)(2,1)S(1)}, bf16[640,512]{1,0:T(8,128)(2,1)S(1)}, u32[]{:S(2)}, u32[]{:S(2)}) collective-permute-start(bf16[640,512]{1,0:T(8,128)(2,1)S(1)} %get-tuple-element.7.refs_0_), channel_id=1, source_target_pairs={{0,1},{1,0},{2,3},{3,2},{4,5},{5,4},{6,7},{7,6},{8,9},{9,8},{10,11... | collective-permute-start | bytes 1966088 | tf_op jit(solution)/shard_map/ppermute | solution.py:99
  194.6 20.8 %collective-permute-start.23 = (bf16[640,512]{1,0:T(8,128)(2,1)S(1)}, bf16[640,512]{1,0:T(8,128)(2,1)S(1)}, u32[]{:S(2)}, u32[]{:S(2)}) collective-permute-start(bf16[640,512]{1,0:T(8,128)(2,1)S(1)} %collective-permute-done.11.refs_13_), channel_id=1, source_target_pairs={{0,12},{4,0},{8,4},{12,8},{1,13},{5,1},{9,5},{13,9},{2,14},{6,2},{... | collective-permute-start | bytes 1966088 | tf_op jit(solution)/shard_map/ppermute | solution.py:72
  201.4 19.0 %collective-permute-start.19 = (bf16[640,512]{1,0:T(8,128)(2,1)S(1)}, bf16[640,512]{1,0:T(8,128)(2,1)S(1)}, u32[]{:S(2)}, u32[]{:S(2)}) collective-permute-start(bf16[640,512]{1,0:T(8,128)(2,1)S(1)} %collective-permute-done.11.refs_13_), channel_id=1, source_target_pairs={{0,2},{2,0},{1,3},{3,1},{4,6},{6,4},{5,7},{7,5},{8,10},{10,8},{9,1... | collective-permute-start | bytes 1966088 | tf_op jit(solution)/shard_map/ppermute | solution.py:72
  205.8 17.8 %collective-permute-start.13 = (bf16[640,512]{1,0:T(8,128)(2,1)S(1)}, bf16[640,512]{1,0:T(8,128)(2,1)S(1)}, u32[]{:S(2)}, u32[]{:S(2)}) collective-permute-start(bf16[640,512]{1,0:T(8,128)(2,1)S(1)} %collective-permute-done.11.refs_13_), channel_id=1, source_target_pairs={{0,1},{1,0},{2,3},{3,2},{4,5},{5,4},{6,7},{7,6},{8,9},{9,8},{10,11... | collective-permute-start | bytes 1966088 | tf_op jit(solution)/shard_map/ppermute | solution.py:99
  207.9 25.9 %collective-permute-start.15 = (bf16[640,512]{1,0:T(8,128)(2,1)S(1)}, bf16[640,512]{1,0:T(8,128)(2,1)}, u32[]{:S(2)}, u32[]{:S(2)}) collective-permute-start(bf16[640,512]{1,0:T(8,128)(2,1)S(1)} %collective-permute-done.7.refs_9_), channel_id=1, source_target_pairs={{0,2},{2,0},{1,3},{3,1},{4,6},{6,4},{5,7},{7,5},{8,10},{10,8},{9,1... | collective-permute-start | bytes 1966088 | tf_op jit(solution)/shard_map/ppermute | solution.py:72
  208.8 27.4 %collective-permute-start.9 = (bf16[640,512]{1,0:T(8,128)(2,1)S(1)}, bf16[640,512]{1,0:T(8,128)(2,1)S(1)}, u32[]{:S(2)}, u32[]{:S(2)}) collective-permute-start(bf16[640,512]{1,0:T(8,128)(2,1)S(1)} %collective-permute-done.7.refs_9_), channel_id=1, source_target_pairs={{0,1},{1,0},{2,3},{3,2},{4,5},{5,4},{6,7},{7,6},{8,9},{9,8},{10,11... | collective-permute-start | bytes 1966088 | tf_op jit(solution)/shard_map/ppermute | solution.py:99
  215.4 25.8 %collective-permute-start.18 = (bf16[640,512]{1,0:T(8,128)(2,1)S(1)}, bf16[640,512]{1,0:T(8,128)(2,1)}, u32[]{:S(2)}, u32[]{:S(2)}) collective-permute-start(bf16[640,512]{1,0:T(8,128)(2,1)S(1)} %collective-permute-done.2.refs_4_), channel_id=1, source_target_pairs={{0,12},{4,0},{8,4},{12,8},{1,13},{5,1},{9,5},{13,9},{2,14},{6,2},{... | collective-permute-start | bytes 1966088 | tf_op jit(solution)/shard_map/ppermute | solution.py:72
  220.3 22.0 %collective-permute-start.14 = (bf16[640,512]{1,0:T(8,128)(2,1)S(1)}, bf16[640,512]{1,0:T(8,128)(2,1)S(1)}, u32[]{:S(2)}, u32[]{:S(2)}) collective-permute-start(bf16[640,512]{1,0:T(8,128)(2,1)S(1)} %collective-permute-done.2.refs_4_), channel_id=1, source_target_pairs={{0,4},{4,8},{8,12},{12,0},{1,5},{5,9},{9,13},{13,1},{2,6},{6,10},{... | collective-permute-start | bytes 1966088 | tf_op jit(solution)/shard_map/ppermute | solution.py:72
  224.4 20.1 %collective-permute-start.5 = (bf16[640,512]{1,0:T(8,128)(2,1)S(1)}, bf16[640,512]{1,0:T(8,128)(2,1)S(1)}, u32[]{:S(2)}, u32[]{:S(2)}) collective-permute-start(bf16[640,512]{1,0:T(8,128)(2,1)S(1)} %collective-permute-done.3.refs_5_), channel_id=1, source_target_pairs={{0,1},{1,0},{2,3},{3,2},{4,5},{5,4},{6,7},{7,6},{8,9},{9,8},{10,11... | collective-permute-start | bytes 1966088 | tf_op jit(solution)/shard_map/ppermute | solution.py:99
  233.8 13.0 %collective-permute-start.12 = (bf16[640,512]{1,0:T(8,128)(2,1)S(1)}, bf16[640,512]{1,0:T(8,128)(2,1)S(1)}, u32[]{:S(2)}, u32[]{:S(2)}) collective-permute-start(bf16[640,512]{1,0:T(8,128)(2,1)S(1)} %collective-permute-done.10.refs_12_), channel_id=1, source_target_pairs={{0,1},{1,0},{2,3},{3,2},{4,5},{5,4},{6,7},{7,6},{8,9},{9,8},{10,11... | collective-permute-start | bytes 1966088 | tf_op jit(solution)/shard_map/ppermute | solution.py:99
  237.0 20.8 %collective-permute-start.22 = (bf16[640,512]{1,0:T(8,128)(2,1)S(1)}, bf16[640,512]{1,0:T(8,128)(2,1)}, u32[]{:S(2)}, u32[]{:S(2)}) collective-permute-start(bf16[640,512]{1,0:T(8,128)(2,1)S(1)} %collective-permute-done.6.refs_8_), channel_id=1, source_target_pairs={{0,4},{4,8},{8,12},{12,0},{1,5},{5,9},{9,13},{13,1},{2,6},{6,10},{... | collective-permute-start | bytes 1966088 | tf_op jit(solution)/shard_map/ppermute | solution.py:72
  241.2 18.1 %collective-permute-start.8 = (bf16[640,512]{1,0:T(8,128)(2,1)S(1)}, bf16[640,512]{1,0:T(8,128)(2,1)S(1)}, u32[]{:S(2)}, u32[]{:S(2)}) collective-permute-start(bf16[640,512]{1,0:T(8,128)(2,1)S(1)} %collective-permute-done.6.refs_8_), channel_id=1, source_target_pairs={{0,1},{1,0},{2,3},{3,2},{4,5},{5,4},{6,7},{7,6},{8,9},{9,8},{10,11... | collective-permute-start | bytes 1966088 | tf_op jit(solution)/shard_map/ppermute | solution.py:99
  242.3 18.9 %collective-permute-start.4 = (bf16[640,512]{1,0:T(8,128)(2,1)S(1)}, bf16[640,512]{1,0:T(8,128)(2,1)S(1)}, u32[]{:S(2)}, u32[]{:S(2)}) collective-permute-start(bf16[640,512]{1,0:T(8,128)(2,1)S(1)} %collective-permute-done.2.refs_4_), channel_id=1, source_target_pairs={{0,1},{1,0},{2,3},{3,2},{4,5},{5,4},{6,7},{7,6},{8,9},{9,8},{10,11... | collective-permute-start | bytes 1966088 | tf_op jit(solution)/shard_map/ppermute | solution.py:99
  245.3 16.7 %collective-permute-start.27 = (bf16[320,512]{1,0:T(8,128)(2,1)S(1)}, bf16[320,512]{1,0:T(8,128)(2,1)S(1)}, u32[]{:S(2)}, u32[]{:S(2)}) collective-permute-start(bf16[320,512]{1,0:T(8,128)(2,1)S(1)} %slice.25), channel_id=1, source_target_pairs={{0,12},{4,0},{8,4},{12,8},{1,13},{5,1},{9,5},{13,9},{2,14},{6,2},{... | collective-permute-start | bytes 983048 | tf_op jit(solution)/shard_map/ppermute | solution.py:72
  247.6 17.3 %collective-permute-start.26 = (bf16[320,512]{1,0:T(8,128)(2,1)S(1)}, bf16[320,512]{1,0:T(8,128)(2,1)S(1)}, u32[]{:S(2)}, u32[]{:S(2)}) collective-permute-start(bf16[320,512]{1,0:T(8,128)(2,1)S(1)} %slice.24), channel_id=1, source_target_pairs={{0,4},{4,8},{8,12},{12,0},{1,5},{5,9},{9,13},{13,1},{2,6},{6,10},{... | collective-permute-start | bytes 983048 | tf_op jit(solution)/shard_map/ppermute | solution.py:72
  257.9 15.6 %collective-permute-start.28 = (bf16[640,512]{1,0:T(8,128)(2,1)S(1)}, bf16[640,512]{1,0:T(8,128)(2,1)}, u32[]{:S(2)}, u32[]{:S(2)}) collective-permute-start(bf16[640,512]{1,0:T(8,128)(2,1)S(1)} %collective-permute-done.23.refs_25_), channel_id=1, source_target_pairs={{0,2},{2,0},{1,3},{3,1},{4,6},{6,4},{5,7},{7,5},{8,10},{10,8},{9,1... | collective-permute-start | bytes 1966088 | tf_op jit(solution)/shard_map/ppermute | solution.py:72
  260.2 15.0 %collective-permute-start.25 = (bf16[640,512]{1,0:T(8,128)(2,1)S(1)}, bf16[640,512]{1,0:T(8,128)(2,1)S(1)}, u32[]{:S(2)}, u32[]{:S(2)}) collective-permute-start(bf16[640,512]{1,0:T(8,128)(2,1)S(1)} %collective-permute-done.23.refs_25_), channel_id=1, source_target_pairs={{0,1},{1,0},{2,3},{3,2},{4,5},{5,4},{6,7},{7,6},{8,9},{9,8},{10,11... | collective-permute-start | bytes 1966088 | tf_op jit(solution)/shard_map/ppermute | solution.py:99
  262.1 13.2 %collective-permute-start.21 = (bf16[640,512]{1,0:T(8,128)(2,1)S(1)}, bf16[640,512]{1,0:T(8,128)(2,1)S(1)}, u32[]{:S(2)}, u32[]{:S(2)}) collective-permute-start(bf16[640,512]{1,0:T(8,128)(2,1)S(1)} %collective-permute-done.19.refs_21_), channel_id=1, source_target_pairs={{0,1},{1,0},{2,3},{3,2},{4,5},{5,4},{6,7},{7,6},{8,9},{9,8},{10,11... | collective-permute-start | bytes 1966088 | tf_op jit(solution)/shard_map/ppermute | solution.py:99
  262.1 4.0 %collective-permute-start.30 = (bf16[320,512]{1,0:T(8,128)(2,1)S(1)}, bf16[320,512]{1,0:T(8,128)(2,1)S(1)}, u32[]{:S(2)}, u32[]{:S(2)}) collective-permute-start(bf16[320,512]{1,0:T(8,128)(2,1)S(1)} %collective-permute-done.27.refs_29_), channel_id=1, source_target_pairs={{0,1},{1,0},{2,3},{3,2},{4,5},{5,4},{6,7},{7,6},{8,9},{9,8},{10,11... | collective-permute-start | bytes 983048 | tf_op jit(solution)/shard_map/ppermute | solution.py:99
  266.8 10.3 %collective-permute-start.20 = (bf16[640,512]{1,0:T(8,128)(2,1)}, bf16[640,512]{1,0:T(8,128)(2,1)}, u32[]{:S(2)}, u32[]{:S(2)}) collective-permute-start(bf16[640,512]{1,0:T(8,128)(2,1)} %collective-permute-done.18.refs_20_), channel_id=1, source_target_pairs={{0,1},{1,0},{2,3},{3,2},{4,5},{5,4},{6,7},{7,6},{8,9},{9,8},{10,11... | collective-permute-start | bytes 1966088 | tf_op jit(solution)/shard_map/ppermute | solution.py:99
  267.6 9.3 %collective-permute-start.17 = (bf16[640,512]{1,0:T(8,128)(2,1)}, bf16[640,512]{1,0:T(8,128)(2,1)}, u32[]{:S(2)}, u32[]{:S(2)}) collective-permute-start(bf16[640,512]{1,0:T(8,128)(2,1)} %collective-permute-done.15.refs_17_), channel_id=1, source_target_pairs={{0,1},{1,0},{2,3},{3,2},{4,5},{5,4},{6,7},{7,6},{8,9},{9,8},{10,11... | collective-permute-start | bytes 1966088 | tf_op jit(solution)/shard_map/ppermute | solution.py:99
  273.5 3.7 %collective-permute-start.24 = (bf16[640,512]{1,0:T(8,128)(2,1)}, bf16[640,512]{1,0:T(8,128)(2,1)}, u32[]{:S(2)}, u32[]{:S(2)}) collective-permute-start(bf16[640,512]{1,0:T(8,128)(2,1)} %collective-permute-done.22.refs_24_), channel_id=1, source_target_pairs={{0,1},{1,0},{2,3},{3,2},{4,5},{5,4},{6,7},{7,6},{8,9},{9,8},{10,11... | collective-permute-start | bytes 1966088 | tf_op jit(solution)/shard_map/ppermute | solution.py:99
  275.1 3.0 collective-permute-start.16
  275.3 3.8 %collective-permute-start.31 = (bf16[640,512]{1,0:T(8,128)(2,1)}, bf16[640,512]{1,0:T(8,128)(2,1)}, u32[]{:S(2)}, u32[]{:S(2)}) collective-permute-start(bf16[640,512]{1,0:T(8,128)(2,1)} %collective-permute-done.28.refs_30_), channel_id=1, source_target_pairs={{0,1},{1,0},{2,3},{3,2},{4,5},{5,4},{6,7},{7,6},{8,9},{9,8},{10,11... | collective-permute-start | bytes 1966088 | tf_op jit(solution)/shard_map/ppermute | solution.py:99
  (38 other events, 315.0 us)

commit v5 on v4

--- a/solution.py
+++ b/solution.py
@@ -13,9 +13,9 @@
 HEAD_DIM = 128
 X = 4
 Q_COLS = Q_HEADS * HEAD_DIM
-AXES = ("x", "zl", "zh", "c", "y")
+AXES = ("zl", "zh", "x", "c", "y")
 SIZES = {"zh": 2, "y": 4, "x": X, "zl": 2, "c": 2}
-SPLIT = 40
+SPLIT = 42
 NEAR = (0, 0), (0, 1), (3, 0), (1, 0)
 REST = (3, 1), (1, 1), (2, 0), (2, 1)
 VMEM_BYTES = 40 * 1024 * 1024
@@ -114,7 +114,7 @@
     flat = [value for pieces in shards for value in pieces]
     steps = len(shards) // 2
     most = max(
-        len(shards[2 * k]) + len(shards[2 * k + 1]) + 2 for k in range(steps)
+        len(shards[2 * k]) + len(shards[2 * k + 1]) + 4 for k in range(steps)
     )
 
     def body(order_ref, *refs):
@@ -132,8 +132,10 @@
                 device = order_ref[n]
                 pick = {"zh": device // 8, "y": device // 2 % 4}
                 pick["x"] = pl.ds(device % 2 * 2, 2)
-                source = w.at[tuple(pick.get(name, slice(None)) for name in AXES)]
-                out.append((source, w_buf.at[slot, n % 2]))
+                for zl in range(2):
+                    pick["zl"] = zl
+                    source = w.at[tuple(pick.get(name, slice(None)) for name in AXES)]
+                    out.append((source, w_buf.at[slot, n % 2, slice(None), zl]))
                 first = 0
                 for value in shards[n]:
                     to = h_buf.at[slot, pl.ds(first, value.shape[0]), pl.ds(col, feats)]

time: 322 us -> 326 us (1.012)
  waiting for transfers between devices: 193 us -> 208 us
  starting transfers between devices: 59.9 us -> 49 us
    ppermute x15, waiting for transfers between devices: 191 us -> 207 us  [move(): return lax.ppermute(value, axis, pairs)]
    ppermute x15, starting transfers between devices: 27 us -> 11.6 us  [move(): return lax.ppermute(value, axis, pairs)]
    ppermute x17, starting transfers between devices: 21.7 us -> 26.3 us  [both(): out[-1].append(lax.ppermute(piece, 'c', [(0, 1), (1, 0)]))]
    unnamed x74 -> x70, local copies, waits for them, and re-layouts: 28.5 us -> 27.5 us
  transfers between devices with their start and end apart: 33 -> 33, of which waited for: 12 -> 8; matrix products, arithmetic and copies ran while one was open for 1% -> 1% of each run, Pallas kernels for 0% -> 0%
where the time goes in v5:
time: 326 us; the launch traced here: 323 us
  waiting for transfers between devices  208 us (64%)
  starting transfers between devices  49 us (15%)
  Pallas kernels  34.5 us (11%)
  local copies, waits for them, and re-layouts  30.2 us (9%)
    ppermute x15, waiting for transfers between devices, move(): return lax.ppermute(value, axis, pairs)  207 us
    unnamed x70, local copies, waits for them, and re-layouts  27.5 us
    ppermute x17, starting transfers between devices, both(): out[-1].append(lax.ppermute(piece, 'c', [(0, 1), (1, 0)]))  26.3 us
    pallas_call x1, Pallas kernels, project(): pl.pallas_call(body, grid_spec=pltpu.PrefetchScalarGridSpec(num_scalar_pr...  22.8 us
    pallas_call x1, Pallas kernels, regroup(): pl.pallas_call(body, grid_spec=pltpu.PrefetchScalarGridSpec(num_scalar_pr...  11.7 us
    ppermute x15, starting transfers between devices, move(): return lax.ppermute(value, axis, pairs)  11.6 us
    all_to_all x1, starting transfers between devices, step(): lax.all_to_all(sending.reshape(-1, *sending.shape[5:]), AXES, split_axis=...  11.2 us
  transfers between devices with their start and end apart: 33, of which 8 were waited for; matrix products, arithmetic and copies ran while one was open for 1% of the time, Pallas kernels for 0%

profile of v5, /device:TPU:5, one launch (start us, length us, event | category | flops | bytes accessed | tf_op | source)
XLA Modules:
  0.0 322.7 jit_solution(9135925906644765527)
XLA Ops:
  0.6 11.7 %regroup.1 = bf16[2,2,4,2,4,64,768]{6,5,4,3,2,1,0:T(8,128)(2,1)} custom-call(s32[16]{0:T(128)} %table.1, bf16[8,64,10240]{2,1,0:T(8,128)(2,1)} %src.1), custom_call_target="tpu_custom_call" | custom-call | tf_op jit(solution)/shard_map/regroup/pallas_call | solution.py:53
  12.4 11.2 %all-to-all-start = ((bf16[128,64,768]{2,1,0:T(8,128)(2,1)}), bf16[128,64,768]{2,1,0:T(8,128)(2,1)}, u32[]{:S(2)}, u32[]{:S(2)}) async-start(bf16[128,64,768]{2,1,0:T(8,128)(2,1)} %bitcast.10), calls=%async_computation | async-start | bytes 25165824 | tf_op jit(solution)/shard_map/all_to_all | solution.py:225
  24.0 1.2 collective-permute-start.7
  25.1 1.3 collective-permute-start.3
  26.9 1.5 collective-permute-start.1
  28.4 159.6 %collective-permute-done.11.refs_13_ = bf16[608,512]{1,0:T(8,128)(2,1)S(1)} collective-permute-done((bf16[608,512]{1,0:T(8,128)(2,1)S(1)}, bf16[608,512]{1,0:T(8,128)(2,1)S(1)}, u32[]{:S(2)}, u32[]{:S(2)}) %collective-permute-start.11) | collective-permute-done | bytes 622624 | tf_op jit(solution)/shard_map/ppermute | solution.py:72
  188.0 1.7 collective-permute-start.2
  189.7 1.8 collective-permute-start
  192.3 1.7 collective-permute-start.23
  194.0 8.7 %collective-permute-done.10.refs_12_ = bf16[672,512]{1,0:T(8,128)(2,1)S(1)} collective-permute-done((bf16[672,512]{1,0:T(8,128)(2,1)S(1)}, bf16[672,512]{1,0:T(8,128)(2,1)S(1)}, u32[]{:S(2)}, u32[]{:S(2)}) %collective-permute-start.10) | collective-permute-done | bytes 688160 | tf_op jit(solution)/shard_map/ppermute | solution.py:72
  202.7 1.6 collective-permute-start.19
  204.3 1.8 collective-permute-start.13
  206.1 1.3 collective-permute-start.15
  208.7 7.3 %collective-permute-done.23.refs_25_ = bf16[608,512]{1,0:T(8,128)(2,1)S(1)} collective-permute-done((bf16[608,512]{1,0:T(8,128)(2,1)S(1)}, bf16[608,512]{1,0:T(8,128)(2,1)S(1)}, u32[]{:S(2)}, u32[]{:S(2)}) %collective-permute-start.23) | collective-permute-done | bytes 622624 | tf_op jit(solution)/shard_map/ppermute | solution.py:72
  219.1 4.9 %collective-permute-start.12 = (bf16[672,512]{1,0:T(8,128)(2,1)S(1)}, bf16[672,512]{1,0:T(8,128)(2,1)S(1)}, u32[]{:S(2)}, u32[]{:S(2)}) collective-permute-start(bf16[672,512]{1,0:T(8,128)(2,1)S(1)} %collective-permute-done.10.refs_12_), channel_id=1, source_target_pairs={{0,1},{1,0},{2,3},{3,2},{4,5},{5,4},{6,7},{7,6},{8,9},{9,8},{10,11... | collective-permute-start | bytes 2064392 | tf_op jit(solution)/shard_map/ppermute | solution.py:99
  224.0 6.7 %collective-permute-done.15.refs_17_ = bf16[608,512]{1,0:T(8,128)(2,1)S(1)} collective-permute-done((bf16[608,512]{1,0:T(8,128)(2,1)S(1)}, bf16[608,512]{1,0:T(8,128)(2,1)S(1)}, u32[]{:S(2)}, u32[]{:S(2)}) %collective-permute-start.15) | collective-permute-done | bytes 622624 | tf_op jit(solution)/shard_map/ppermute | solution.py:72
  231.5 2.1 collective-permute-start.8
  234.4 1.4 collective-permute-start.4
  237.3 8.4 %collective-permute-done.22.refs_24_ = bf16[672,512]{1,0:T(8,128)(2,1)} collective-permute-done((bf16[672,512]{1,0:T(8,128)(2,1)S(1)}, bf16[672,512]{1,0:T(8,128)(2,1)}, u32[]{:S(2)}, u32[]{:S(2)}) %collective-permute-start.22) | collective-permute-done | bytes 688160 | tf_op jit(solution)/shard_map/ppermute | solution.py:72
  245.7 1.2 collective-permute-start.28
  246.9 6.1 %collective-permute-start.25 = (bf16[608,512]{1,0:T(8,128)(2,1)S(1)}, bf16[608,512]{1,0:T(8,128)(2,1)S(1)}, u32[]{:S(2)}, u32[]{:S(2)}) collective-permute-start(bf16[608,512]{1,0:T(8,128)(2,1)S(1)} %collective-permute-done.23.refs_25_), channel_id=1, source_target_pairs={{0,1},{1,0},{2,3},{3,2},{4,5},{5,4},{6,7},{7,6},{8,9},{9,8},{10,11... | collective-permute-start | bytes 1867784 | tf_op jit(solution)/shard_map/ppermute | solution.py:99
  253.8 6.7 %collective-permute-done.14.refs_16_ = bf16[672,512]{1,0:T(8,128)(2,1)} collective-permute-done((bf16[672,512]{1,0:T(8,128)(2,1)S(1)}, bf16[672,512]{1,0:T(8,128)(2,1)}, u32[]{:S(2)}, u32[]{:S(2)}) %collective-permute-start.14) | collective-permute-done | bytes 688160 | tf_op jit(solution)/shard_map/ppermute | solution.py:72
  260.5 2.9 collective-permute-start.21
  266.2 9.2 %collective-permute-done.26.refs_28_ = bf16[336,512]{1,0:T(8,128)(2,1)} collective-permute-done((bf16[336,512]{1,0:T(8,128)(2,1)S(1)}, bf16[336,512]{1,0:T(8,128)(2,1)}, u32[]{:S(2)}, u32[]{:S(2)}) %collective-permute-start.26) | collective-permute-done | bytes 344096 | tf_op jit(solution)/shard_map/ppermute | solution.py:72
  275.4 1.4 collective-permute-start.20
  282.5 1.3 collective-permute-done.29.refs_31_
  284.9 1.1 copy-done.3
  285.9 1.1 copy-done.5
  287.0 1.1 copy-done.7
  288.1 1.1 copy-done.9
  293.5 1.1 copy-done.19
  299.7 22.8 %project.1 = (bf16[1280,512]{1,0:T(8,128)(2,1)}, bf16[1280,256]{1,0:T(8,128)(2,1)}) custom-call(s32[16]{0:T(128)S(1)} %dynamic-slice_bitcast_fusion.order_ref, bf16[672,512]{1,0:T(8,128)(2,1)S(1)} %slice_bitcast_fusion.refs_0_, bf16[608,512]{1,0:T(8,128)(2,1)S(1)} %slice_bitcast_fusion.1.refs_1_, bf16[672,512]{1,0:T(8,128)(2,1)S(1)} %collective-permute-done.refs_2_, ...), custom_call_target="tpu_custom_call" | custom-call | tf_op jit(solution)/shard_map/project/pallas_call | solution.py:205
  (111 shorter events, 29.0 us)
Async XLA Ops:
  12.4 271.4 %all-to-all-start = ((bf16[128,64,768]{2,1,0:T(8,128)(2,1)}), bf16[128,64,768]{2,1,0:T(8,128)(2,1)}, u32[]{:S(2)}, u32[]{:S(2)}) async-start(bf16[128,64,768]{2,1,0:T(8,128)(2,1)} %bitcast.10), calls=%async_computation | async-start | bytes 25165824 | tf_op jit(solution)/shard_map/all_to_all | solution.py:225
  23.6 164.4 %collective-permute-start.11 = (bf16[608,512]{1,0:T(8,128)(2,1)S(1)}, bf16[608,512]{1,0:T(8,128)(2,1)S(1)}, u32[]{:S(2)}, u32[]{:S(2)}) collective-permute-start(bf16[608,512]{1,0:T(8,128)(2,1)S(1)} %slice_bitcast_fusion.1.refs_1_), channel_id=1, source_target_pairs={{0,12},{4,0},{8,4},{12,8},{1,13},{5,1},{9,5},{13,9},{2,14},{6,2},{... | collective-permute-start | bytes 1867784 | tf_op jit(solution)/shard_map/ppermute | solution.py:72
  24.0 164.0 %collective-permute-start.7 = (bf16[608,512]{1,0:T(8,128)(2,1)S(1)}, bf16[608,512]{1,0:T(8,128)(2,1)S(1)}, u32[]{:S(2)}, u32[]{:S(2)}) collective-permute-start(bf16[608,512]{1,0:T(8,128)(2,1)S(1)} %slice_bitcast_fusion.1.refs_1_), channel_id=1, source_target_pairs={{0,4},{4,8},{8,12},{12,0},{1,5},{5,9},{9,13},{13,1},{2,6},{6,10},{... | collective-permute-start | bytes 1867784 | tf_op jit(solution)/shard_map/ppermute | solution.py:72
  25.1 164.5 %collective-permute-start.3 = (bf16[608,512]{1,0:T(8,128)(2,1)S(1)}, bf16[608,512]{1,0:T(8,128)(2,1)S(1)}, u32[]{:S(2)}, u32[]{:S(2)}) collective-permute-start(bf16[608,512]{1,0:T(8,128)(2,1)S(1)} %slice_bitcast_fusion.1.refs_1_), channel_id=1, source_target_pairs={{0,2},{2,0},{1,3},{3,1},{4,6},{6,4},{5,7},{7,5},{8,10},{10,8},{9,1... | collective-permute-start | bytes 1867784 | tf_op jit(solution)/shard_map/ppermute | solution.py:72
  26.5 176.2 %collective-permute-start.10 = (bf16[672,512]{1,0:T(8,128)(2,1)S(1)}, bf16[672,512]{1,0:T(8,128)(2,1)S(1)}, u32[]{:S(2)}, u32[]{:S(2)}) collective-permute-start(bf16[672,512]{1,0:T(8,128)(2,1)S(1)} %slice_bitcast_fusion.refs_0_), channel_id=1, source_target_pairs={{0,12},{4,0},{8,4},{12,8},{1,13},{5,1},{9,5},{13,9},{2,14},{6,2},{... | collective-permute-start | bytes 2064392 | tf_op jit(solution)/shard_map/ppermute | solution.py:72
  26.9 164.6 %collective-permute-start.1 = (bf16[608,512]{1,0:T(8,128)(2,1)S(1)}, bf16[608,512]{1,0:T(8,128)(2,1)S(1)}, u32[]{:S(2)}, u32[]{:S(2)}) collective-permute-start(bf16[608,512]{1,0:T(8,128)(2,1)S(1)} %slice_bitcast_fusion.1.refs_1_), channel_id=1, source_target_pairs={{0,1},{1,0},{2,3},{3,2},{4,5},{5,4},{6,7},{7,6},{8,9},{9,8},{10,11... | collective-permute-start | bytes 1867784 | tf_op jit(solution)/shard_map/ppermute | solution.py:99
  188.0 16.4 %collective-permute-start.6 = (bf16[672,512]{1,0:T(8,128)(2,1)S(1)}, bf16[672,512]{1,0:T(8,128)(2,1)S(1)}, u32[]{:S(2)}, u32[]{:S(2)}) collective-permute-start(bf16[672,512]{1,0:T(8,128)(2,1)S(1)} %slice_bitcast_fusion.refs_0_), channel_id=1, source_target_pairs={{0,4},{4,8},{8,12},{12,0},{1,5},{5,9},{9,13},{13,1},{2,6},{6,10},{... | collective-permute-start | bytes 2064392 | tf_op jit(solution)/shard_map/ppermute | solution.py:72
  188.0 18.2 %collective-permute-start.2 = (bf16[672,512]{1,0:T(8,128)(2,1)S(1)}, bf16[672,512]{1,0:T(8,128)(2,1)S(1)}, u32[]{:S(2)}, u32[]{:S(2)}) collective-permute-start(bf16[672,512]{1,0:T(8,128)(2,1)S(1)} %slice_bitcast_fusion.refs_0_), channel_id=1, source_target_pairs={{0,2},{2,0},{1,3},{3,1},{4,6},{6,4},{5,7},{7,5},{8,10},{10,8},{9,1... | collective-permute-start | bytes 2064392 | tf_op jit(solution)/shard_map/ppermute | solution.py:72
  189.7 17.8 %collective-permute-start = (bf16[672,512]{1,0:T(8,128)(2,1)S(1)}, bf16[672,512]{1,0:T(8,128)(2,1)S(1)}, u32[]{:S(2)}, u32[]{:S(2)}) collective-permute-start(bf16[672,512]{1,0:T(8,128)(2,1)S(1)} %slice_bitcast_fusion.refs_0_), channel_id=1, source_target_pairs={{0,1},{1,0},{2,3},{3,2},{4,5},{5,4},{6,7},{7,6},{8,9},{9,8},{10,11... | collective-permute-start | bytes 2064392 | tf_op jit(solution)/shard_map/ppermute | solution.py:99
  192.3 23.7 %collective-permute-start.23 = (bf16[608,512]{1,0:T(8,128)(2,1)S(1)}, bf16[608,512]{1,0:T(8,128)(2,1)S(1)}, u32[]{:S(2)}, u32[]{:S(2)}) collective-permute-start(bf16[608,512]{1,0:T(8,128)(2,1)S(1)} %collective-permute-done.11.refs_13_), channel_id=1, source_target_pairs={{0,12},{4,0},{8,4},{12,8},{1,13},{5,1},{9,5},{13,9},{2,14},{6,2},{... | collective-permute-start | bytes 1867784 | tf_op jit(solution)/shard_map/ppermute | solution.py:72
  202.7 15.1 %collective-permute-start.19 = (bf16[608,512]{1,0:T(8,128)(2,1)S(1)}, bf16[608,512]{1,0:T(8,128)(2,1)S(1)}, u32[]{:S(2)}, u32[]{:S(2)}) collective-permute-start(bf16[608,512]{1,0:T(8,128)(2,1)S(1)} %collective-permute-done.11.refs_13_), channel_id=1, source_target_pairs={{0,2},{2,0},{1,3},{3,1},{4,6},{6,4},{5,7},{7,5},{8,10},{10,8},{9,1... | collective-permute-start | bytes 1867784 | tf_op jit(solution)/shard_map/ppermute | solution.py:72
  204.3 13.9 %collective-permute-start.13 = (bf16[608,512]{1,0:T(8,128)(2,1)S(1)}, bf16[608,512]{1,0:T(8,128)(2,1)S(1)}, u32[]{:S(2)}, u32[]{:S(2)}) collective-permute-start(bf16[608,512]{1,0:T(8,128)(2,1)S(1)} %collective-permute-done.11.refs_13_), channel_id=1, source_target_pairs={{0,1},{1,0},{2,3},{3,2},{4,5},{5,4},{6,7},{7,6},{8,9},{9,8},{10,11... | collective-permute-start | bytes 1867784 | tf_op jit(solution)/shard_map/ppermute | solution.py:99
  206.1 24.5 %collective-permute-start.15 = (bf16[608,512]{1,0:T(8,128)(2,1)S(1)}, bf16[608,512]{1,0:T(8,128)(2,1)S(1)}, u32[]{:S(2)}, u32[]{:S(2)}) collective-permute-start(bf16[608,512]{1,0:T(8,128)(2,1)S(1)} %collective-permute-done.7.refs_9_), channel_id=1, source_target_pairs={{0,2},{2,0},{1,3},{3,1},{4,6},{6,4},{5,7},{7,5},{8,10},{10,8},{9,1... | collective-permute-start | bytes 1867784 | tf_op jit(solution)/shard_map/ppermute | solution.py:72
  207.4 23.3 %collective-permute-start.9 = (bf16[608,512]{1,0:T(8,128)(2,1)S(1)}, bf16[608,512]{1,0:T(8,128)(2,1)S(1)}, u32[]{:S(2)}, u32[]{:S(2)}) collective-permute-start(bf16[608,512]{1,0:T(8,128)(2,1)S(1)} %collective-permute-done.7.refs_9_), channel_id=1, source_target_pairs={{0,1},{1,0},{2,3},{3,2},{4,5},{5,4},{6,7},{7,6},{8,9},{9,8},{10,11... | collective-permute-start | bytes 1867784 | tf_op jit(solution)/shard_map/ppermute | solution.py:99
  216.0 17.5 %collective-permute-start.5 = (bf16[608,512]{1,0:T(8,128)(2,1)S(1)}, bf16[608,512]{1,0:T(8,128)(2,1)S(1)}, u32[]{:S(2)}, u32[]{:S(2)}) collective-permute-start(bf16[608,512]{1,0:T(8,128)(2,1)S(1)} %collective-permute-done.3.refs_5_), channel_id=1, source_target_pairs={{0,1},{1,0},{2,3},{3,2},{4,5},{5,4},{6,7},{7,6},{8,9},{9,8},{10,11... | collective-permute-start | bytes 1867784 | tf_op jit(solution)/shard_map/ppermute | solution.py:99
  217.8 16.6 %collective-permute-start.18 = (bf16[672,512]{1,0:T(8,128)(2,1)S(1)}, bf16[672,512]{1,0:T(8,128)(2,1)}, u32[]{:S(2)}, u32[]{:S(2)}) collective-permute-start(bf16[672,512]{1,0:T(8,128)(2,1)S(1)} %collective-permute-done.2.refs_4_), channel_id=1, source_target_pairs={{0,12},{4,0},{8,4},{12,8},{1,13},{5,1},{9,5},{13,9},{2,14},{6,2},{... | collective-permute-start | bytes 2064392 | tf_op jit(solution)/shard_map/ppermute | solution.py:72
  219.1 17.8 %collective-permute-start.12 = (bf16[672,512]{1,0:T(8,128)(2,1)S(1)}, bf16[672,512]{1,0:T(8,128)(2,1)S(1)}, u32[]{:S(2)}, u32[]{:S(2)}) collective-permute-start(bf16[672,512]{1,0:T(8,128)(2,1)S(1)} %collective-permute-done.10.refs_12_), channel_id=1, source_target_pairs={{0,1},{1,0},{2,3},{3,2},{4,5},{5,4},{6,7},{7,6},{8,9},{9,8},{10,11... | collective-permute-start | bytes 2064392 | tf_op jit(solution)/shard_map/ppermute | solution.py:99
  230.7 15.0 %collective-permute-start.22 = (bf16[672,512]{1,0:T(8,128)(2,1)S(1)}, bf16[672,512]{1,0:T(8,128)(2,1)}, u32[]{:S(2)}, u32[]{:S(2)}) collective-permute-start(bf16[672,512]{1,0:T(8,128)(2,1)S(1)} %collective-permute-done.6.refs_8_), channel_id=1, source_target_pairs={{0,4},{4,8},{8,12},{12,0},{1,5},{5,9},{9,13},{13,1},{2,6},{6,10},{... | collective-permute-start | bytes 2064392 | tf_op jit(solution)/shard_map/ppermute | solution.py:72
  231.5 15.4 %collective-permute-start.8 = (bf16[672,512]{1,0:T(8,128)(2,1)S(1)}, bf16[672,512]{1,0:T(8,128)(2,1)S(1)}, u32[]{:S(2)}, u32[]{:S(2)}) collective-permute-start(bf16[672,512]{1,0:T(8,128)(2,1)S(1)} %collective-permute-done.6.refs_8_), channel_id=1, source_target_pairs={{0,1},{1,0},{2,3},{3,2},{4,5},{5,4},{6,7},{7,6},{8,9},{9,8},{10,11... | collective-permute-start | bytes 2064392 | tf_op jit(solution)/shard_map/ppermute | solution.py:99
  234.4 26.0 %collective-permute-start.14 = (bf16[672,512]{1,0:T(8,128)(2,1)S(1)}, bf16[672,512]{1,0:T(8,128)(2,1)}, u32[]{:S(2)}, u32[]{:S(2)}) collective-permute-start(bf16[672,512]{1,0:T(8,128)(2,1)S(1)} %collective-permute-done.2.refs_4_), channel_id=1, source_target_pairs={{0,4},{4,8},{8,12},{12,0},{1,5},{5,9},{9,13},{13,1},{2,6},{6,10},{... | collective-permute-start | bytes 2064392 | tf_op jit(solution)/shard_map/ppermute | solution.py:72
  234.4 29.8 %collective-permute-start.4 = (bf16[672,512]{1,0:T(8,128)(2,1)S(1)}, bf16[672,512]{1,0:T(8,128)(2,1)S(1)}, u32[]{:S(2)}, u32[]{:S(2)}) collective-permute-start(bf16[672,512]{1,0:T(8,128)(2,1)S(1)} %collective-permute-done.2.refs_4_), channel_id=1, source_target_pairs={{0,1},{1,0},{2,3},{3,2},{4,5},{5,4},{6,7},{7,6},{8,9},{9,8},{10,11... | collective-permute-start | bytes 2064392 | tf_op jit(solution)/shard_map/ppermute | solution.py:99
  236.8 29.2 %collective-permute-start.27 = (bf16[336,512]{1,0:T(8,128)(2,1)S(1)}, bf16[336,512]{1,0:T(8,128)(2,1)S(1)}, u32[]{:S(2)}, u32[]{:S(2)}) collective-permute-start(bf16[336,512]{1,0:T(8,128)(2,1)S(1)} %slice.25), channel_id=1, source_target_pairs={{0,12},{4,0},{8,4},{12,8},{1,13},{5,1},{9,5},{13,9},{2,14},{6,2},{... | collective-permute-start | bytes 1032200 | tf_op jit(solution)/shard_map/ppermute | solution.py:72
  245.7 31.0 %collective-permute-start.28 = (bf16[608,512]{1,0:T(8,128)(2,1)S(1)}, bf16[608,512]{1,0:T(8,128)(2,1)}, u32[]{:S(2)}, u32[]{:S(2)}) collective-permute-start(bf16[608,512]{1,0:T(8,128)(2,1)S(1)} %collective-permute-done.23.refs_25_), channel_id=1, source_target_pairs={{0,2},{2,0},{1,3},{3,1},{4,6},{6,4},{5,7},{7,5},{8,10},{10,8},{9,1... | collective-permute-start | bytes 1867784 | tf_op jit(solution)/shard_map/ppermute | solution.py:72
  246.9 30.6 %collective-permute-start.25 = (bf16[608,512]{1,0:T(8,128)(2,1)S(1)}, bf16[608,512]{1,0:T(8,128)(2,1)S(1)}, u32[]{:S(2)}, u32[]{:S(2)}) collective-permute-start(bf16[608,512]{1,0:T(8,128)(2,1)S(1)} %collective-permute-done.23.refs_25_), channel_id=1, source_target_pairs={{0,1},{1,0},{2,3},{3,2},{4,5},{5,4},{6,7},{7,6},{8,9},{9,8},{10,11... | collective-permute-start | bytes 1867784 | tf_op jit(solution)/shard_map/ppermute | solution.py:99
  260.5 18.3 %collective-permute-start.21 = (bf16[608,512]{1,0:T(8,128)(2,1)S(1)}, bf16[608,512]{1,0:T(8,128)(2,1)S(1)}, u32[]{:S(2)}, u32[]{:S(2)}) collective-permute-start(bf16[608,512]{1,0:T(8,128)(2,1)S(1)} %collective-permute-done.19.refs_21_), channel_id=1, source_target_pairs={{0,1},{1,0},{2,3},{3,2},{4,5},{5,4},{6,7},{7,6},{8,9},{9,8},{10,11... | collective-permute-start | bytes 1867784 | tf_op jit(solution)/shard_map/ppermute | solution.py:99
  264.2 15.5 %collective-permute-start.17 = (bf16[608,512]{1,0:T(8,128)(2,1)S(1)}, bf16[608,512]{1,0:T(8,128)(2,1)S(1)}, u32[]{:S(2)}, u32[]{:S(2)}) collective-permute-start(bf16[608,512]{1,0:T(8,128)(2,1)S(1)} %collective-permute-done.15.refs_17_), channel_id=1, source_target_pairs={{0,1},{1,0},{2,3},{3,2},{4,5},{5,4},{6,7},{7,6},{8,9},{9,8},{10,11... | collective-permute-start | bytes 1867784 | tf_op jit(solution)/shard_map/ppermute | solution.py:99
  266.1 9.3 %collective-permute-start.26 = (bf16[336,512]{1,0:T(8,128)(2,1)S(1)}, bf16[336,512]{1,0:T(8,128)(2,1)}, u32[]{:S(2)}, u32[]{:S(2)}) collective-permute-start(bf16[336,512]{1,0:T(8,128)(2,1)S(1)} %slice.24), channel_id=1, source_target_pairs={{0,4},{4,8},{8,12},{12,0},{1,5},{5,9},{9,13},{13,1},{2,6},{6,10},{... | collective-permute-start | bytes 1032200 | tf_op jit(solution)/shard_map/ppermute | solution.py:72
  275.4 8.4 %collective-permute-start.20 = (bf16[672,512]{1,0:T(8,128)(2,1)}, bf16[672,512]{1,0:T(8,128)(2,1)}, u32[]{:S(2)}, u32[]{:S(2)}) collective-permute-start(bf16[672,512]{1,0:T(8,128)(2,1)} %collective-permute-done.18.refs_20_), channel_id=1, source_target_pairs={{0,1},{1,0},{2,3},{3,2},{4,5},{5,4},{6,7},{7,6},{8,9},{9,8},{10,11... | collective-permute-start | bytes 2064392 | tf_op jit(solution)/shard_map/ppermute | solution.py:99
  276.7 4.3 %collective-permute-start.30 = (bf16[336,512]{1,0:T(8,128)(2,1)S(1)}, bf16[336,512]{1,0:T(8,128)(2,1)S(1)}, u32[]{:S(2)}, u32[]{:S(2)}) collective-permute-start(bf16[336,512]{1,0:T(8,128)(2,1)S(1)} %collective-permute-done.27.refs_29_), channel_id=1, source_target_pairs={{0,1},{1,0},{2,3},{3,2},{4,5},{5,4},{6,7},{7,6},{8,9},{9,8},{10,11... | collective-permute-start | bytes 1032200 | tf_op jit(solution)/shard_map/ppermute | solution.py:99
  278.3 5.5 %collective-permute-start.24 = (bf16[672,512]{1,0:T(8,128)(2,1)}, bf16[672,512]{1,0:T(8,128)(2,1)}, u32[]{:S(2)}, u32[]{:S(2)}) collective-permute-start(bf16[672,512]{1,0:T(8,128)(2,1)} %collective-permute-done.22.refs_24_), channel_id=1, source_target_pairs={{0,1},{1,0},{2,3},{3,2},{4,5},{5,4},{6,7},{7,6},{8,9},{9,8},{10,11... | collective-permute-start | bytes 2064392 | tf_op jit(solution)/shard_map/ppermute | solution.py:99
  279.7 4.1 %collective-permute-start.16 = (bf16[672,512]{1,0:T(8,128)(2,1)}, bf16[672,512]{1,0:T(8,128)(2,1)}, u32[]{:S(2)}, u32[]{:S(2)}) collective-permute-start(bf16[672,512]{1,0:T(8,128)(2,1)} %collective-permute-done.14.refs_16_), channel_id=1, source_target_pairs={{0,1},{1,0},{2,3},{3,2},{4,5},{5,4},{6,7},{7,6},{8,9},{9,8},{10,11... | collective-permute-start | bytes 2064392 | tf_op jit(solution)/shard_map/ppermute | solution.py:99
  280.5 3.3 %collective-permute-start.31 = (bf16[608,512]{1,0:T(8,128)(2,1)}, bf16[608,512]{1,0:T(8,128)(2,1)}, u32[]{:S(2)}, u32[]{:S(2)}) collective-permute-start(bf16[608,512]{1,0:T(8,128)(2,1)} %collective-permute-done.28.refs_30_), channel_id=1, source_target_pairs={{0,1},{1,0},{2,3},{3,2},{4,5},{5,4},{6,7},{7,6},{8,9},{9,8},{10,11... | collective-permute-start | bytes 1867784 | tf_op jit(solution)/shard_map/ppermute | solution.py:99
  (36 other events, 270.5 us)

commit v6 on v5

--- a/solution.py
+++ b/solution.py
@@ -16,6 +16,7 @@
 AXES = ("zl", "zh", "x", "c", "y")
 SIZES = {"zh": 2, "y": 4, "x": X, "zl": 2, "c": 2}
 SPLIT = 42
+TILES = 4
 NEAR = (0, 0), (0, 1), (3, 0), (1, 0)
 REST = (3, 1), (1, 1), (2, 0), (2, 1)
 VMEM_BYTES = 40 * 1024 * 1024
@@ -120,7 +121,7 @@
     def body(order_ref, *refs):
         pieces, refs = list(refs[: len(flat)]), refs[len(flat) :]
         w, refs = refs[0], refs[1:]
-        q, kv, h_buf, w_buf, sems, total = refs
+        q, kv, h_buf, w_buf, sems, total, q_out, kv_out, out_sems = refs
         k = pl.program_id(0)
 
         def copies(step):
@@ -179,12 +180,22 @@
 
         @pl.when(k == steps - 1)
         def _():
-            done = total[...] + product()
-            q[...] = done[:, :q_width].astype(q.dtype)
-            kv[...] = done[:, q_width:].astype(kv.dtype)
-
-    def whole(k, *_):
-        return (0, 0)
+            outs = []
+            for i in range(TILES):
+                at = slice(i * toks // TILES, (i + 1) * toks // TILES)
+                done = total[at] + jnp.dot(
+                    h_buf[(steps - 1) % 2, at],
+                    w_buf[(steps - 1) % 2].reshape(2 * feats, width),
+                    preferred_element_type=jnp.float32,
+                )
+                q_out[at] = done[:, :q_width].astype(q.dtype)
+                kv_out[at] = done[:, q_width:].astype(kv.dtype)
+                outs.append(pltpu.make_async_copy(q_out.at[at], q.at[at], out_sems.at[0, i]))
+                outs.append(pltpu.make_async_copy(kv_out.at[at], kv.at[at], out_sems.at[1, i]))
+                outs[-2].start()
+                outs[-1].start()
+            for copy in outs:
+                copy.wait()
 
     in_specs = [pl.BlockSpec(memory_space=pl.ANY)] * (len(flat) + 1)
     scratch = [
@@ -192,11 +203,14 @@
         pltpu.VMEM((2, 2, 2, 2, 2, rows, width), jnp.bfloat16),
         pltpu.SemaphoreType.DMA((2, most)),
         pltpu.VMEM((toks, width), jnp.float32),
+        pltpu.VMEM((toks, q_width), jnp.bfloat16),
+        pltpu.VMEM((toks, width - q_width), jnp.bfloat16),
+        pltpu.SemaphoreType.DMA((2, TILES)),
     ]
     args = [order, *flat, weight]
     out_specs = [
-        pl.BlockSpec((toks, q_width), whole),
-        pl.BlockSpec((toks, width - q_width), whole),
+        pl.BlockSpec(memory_space=pl.ANY),
+        pl.BlockSpec(memory_space=pl.ANY),
     ]
     out_shape = [
         jax.ShapeDtypeStruct((toks, q_width), jnp.bfloat16),

time: 326 us -> 325 us (level)
  no operation moved by 1% of the time
where the time goes in v6:
time: 325 us; the launch traced here: 322 us
  waiting for transfers between devices  208 us (64%)
  starting transfers between devices  49 us (15%)
  Pallas kernels  34 us (10%)
  local copies, waits for them, and re-layouts  30.2 us (9%)
    ppermute x15, waiting for transfers between devices, move(): return lax.ppermute(value, axis, pairs)  207 us
    unnamed x70, local copies, waits for them, and re-layouts  27.5 us
    ppermute x17, starting transfers between devices, both(): out[-1].append(lax.ppermute(piece, 'c', [(0, 1), (1, 0)]))  26.3 us
    pallas_call x1, Pallas kernels, project(): pl.pallas_call(body, grid_spec=pltpu.PrefetchScalarGridSpec(num_scalar_pr...  22.3 us
    pallas_call x1, Pallas kernels, regroup(): pl.pallas_call(body, grid_spec=pltpu.PrefetchScalarGridSpec(num_scalar_pr...  11.7 us
    ppermute x15, starting transfers between devices, move(): return lax.ppermute(value, axis, pairs)  11.6 us
    all_to_all x1, starting transfers between devices, step(): lax.all_to_all(sending.reshape(-1, *sending.shape[5:]), AXES, split_axis=...  11.2 us
  transfers between devices with their start and end apart: 33, of which 8 were waited for; matrix products, arithmetic and copies ran while one was open for 1% of the time, Pallas kernels for 0%

profile of v6, /device:TPU:5, one launch (start us, length us, event | category | flops | bytes accessed | tf_op | source)
XLA Modules:
  0.0 322.2 jit_solution(1964652369642235786)
XLA Ops:
  0.6 11.7 %regroup.1 = bf16[2,2,4,2,4,64,768]{6,5,4,3,2,1,0:T(8,128)(2,1)} custom-call(s32[16]{0:T(128)} %table.1, bf16[8,64,10240]{2,1,0:T(8,128)(2,1)} %src.1), custom_call_target="tpu_custom_call" | custom-call | tf_op jit(solution)/shard_map/regroup/pallas_call | solution.py:54
  12.4 11.2 %all-to-all-start = ((bf16[128,64,768]{2,1,0:T(8,128)(2,1)}), bf16[128,64,768]{2,1,0:T(8,128)(2,1)}, u32[]{:S(2)}, u32[]{:S(2)}) async-start(bf16[128,64,768]{2,1,0:T(8,128)(2,1)} %bitcast.10), calls=%async_computation | async-start | bytes 25165824 | tf_op jit(solution)/shard_map/all_to_all | solution.py:239
  24.0 1.2 collective-permute-start.7
  25.1 1.3 collective-permute-start.3
  26.9 1.5 collective-permute-start.1
  28.4 159.6 %collective-permute-done.11.refs_13_ = bf16[608,512]{1,0:T(8,128)(2,1)S(1)} collective-permute-done((bf16[608,512]{1,0:T(8,128)(2,1)S(1)}, bf16[608,512]{1,0:T(8,128)(2,1)S(1)}, u32[]{:S(2)}, u32[]{:S(2)}) %collective-permute-start.11) | collective-permute-done | bytes 622624 | tf_op jit(solution)/shard_map/ppermute | solution.py:73
  188.0 1.7 collective-permute-start.2
  189.7 1.8 collective-permute-start
  192.3 1.7 collective-permute-start.23
  194.0 8.7 %collective-permute-done.10.refs_12_ = bf16[672,512]{1,0:T(8,128)(2,1)S(1)} collective-permute-done((bf16[672,512]{1,0:T(8,128)(2,1)S(1)}, bf16[672,512]{1,0:T(8,128)(2,1)S(1)}, u32[]{:S(2)}, u32[]{:S(2)}) %collective-permute-start.10) | collective-permute-done | bytes 688160 | tf_op jit(solution)/shard_map/ppermute | solution.py:73
  202.7 1.6 collective-permute-start.19
  204.3 1.8 collective-permute-start.13
  206.1 1.3 collective-permute-start.15
  208.7 7.3 %collective-permute-done.23.refs_25_ = bf16[608,512]{1,0:T(8,128)(2,1)S(1)} collective-permute-done((bf16[608,512]{1,0:T(8,128)(2,1)S(1)}, bf16[608,512]{1,0:T(8,128)(2,1)S(1)}, u32[]{:S(2)}, u32[]{:S(2)}) %collective-permute-start.23) | collective-permute-done | bytes 622624 | tf_op jit(solution)/shard_map/ppermute | solution.py:73
  219.1 4.9 %collective-permute-start.12 = (bf16[672,512]{1,0:T(8,128)(2,1)S(1)}, bf16[672,512]{1,0:T(8,128)(2,1)S(1)}, u32[]{:S(2)}, u32[]{:S(2)}) collective-permute-start(bf16[672,512]{1,0:T(8,128)(2,1)S(1)} %collective-permute-done.10.refs_12_), channel_id=1, source_target_pairs={{0,1},{1,0},{2,3},{3,2},{4,5},{5,4},{6,7},{7,6},{8,9},{9,8},{10,11... | collective-permute-start | bytes 2064392 | tf_op jit(solution)/shard_map/ppermute | solution.py:100
  224.0 6.7 %collective-permute-done.15.refs_17_ = bf16[608,512]{1,0:T(8,128)(2,1)S(1)} collective-permute-done((bf16[608,512]{1,0:T(8,128)(2,1)S(1)}, bf16[608,512]{1,0:T(8,128)(2,1)S(1)}, u32[]{:S(2)}, u32[]{:S(2)}) %collective-permute-start.15) | collective-permute-done | bytes 622624 | tf_op jit(solution)/shard_map/ppermute | solution.py:73
  231.5 2.1 collective-permute-start.8
  234.4 1.4 collective-permute-start.4
  237.3 8.4 %collective-permute-done.22.refs_24_ = bf16[672,512]{1,0:T(8,128)(2,1)} collective-permute-done((bf16[672,512]{1,0:T(8,128)(2,1)S(1)}, bf16[672,512]{1,0:T(8,128)(2,1)}, u32[]{:S(2)}, u32[]{:S(2)}) %collective-permute-start.22) | collective-permute-done | bytes 688160 | tf_op jit(solution)/shard_map/ppermute | solution.py:73
  245.7 1.2 collective-permute-start.28
  246.9 6.1 %collective-permute-start.25 = (bf16[608,512]{1,0:T(8,128)(2,1)S(1)}, bf16[608,512]{1,0:T(8,128)(2,1)S(1)}, u32[]{:S(2)}, u32[]{:S(2)}) collective-permute-start(bf16[608,512]{1,0:T(8,128)(2,1)S(1)} %collective-permute-done.23.refs_25_), channel_id=1, source_target_pairs={{0,1},{1,0},{2,3},{3,2},{4,5},{5,4},{6,7},{7,6},{8,9},{9,8},{10,11... | collective-permute-start | bytes 1867784 | tf_op jit(solution)/shard_map/ppermute | solution.py:100
  253.8 6.7 %collective-permute-done.14.refs_16_ = bf16[672,512]{1,0:T(8,128)(2,1)} collective-permute-done((bf16[672,512]{1,0:T(8,128)(2,1)S(1)}, bf16[672,512]{1,0:T(8,128)(2,1)}, u32[]{:S(2)}, u32[]{:S(2)}) %collective-permute-start.14) | collective-permute-done | bytes 688160 | tf_op jit(solution)/shard_map/ppermute | solution.py:73
  260.5 2.9 collective-permute-start.21
  266.2 9.2 %collective-permute-done.26.refs_28_ = bf16[336,512]{1,0:T(8,128)(2,1)} collective-permute-done((bf16[336,512]{1,0:T(8,128)(2,1)S(1)}, bf16[336,512]{1,0:T(8,128)(2,1)}, u32[]{:S(2)}, u32[]{:S(2)}) %collective-permute-start.26) | collective-permute-done | bytes 344096 | tf_op jit(solution)/shard_map/ppermute | solution.py:73
  275.4 1.4 collective-permute-start.20
  282.5 1.3 collective-permute-done.29.refs_31_
  284.9 1.1 copy-done.3
  285.9 1.1 copy-done.5
  287.0 1.1 copy-done.7
  288.1 1.1 copy-done.9
  293.5 1.1 copy-done.19
  299.7 22.3 %project.1 = (bf16[1280,512]{1,0:T(8,128)(2,1)}, bf16[1280,256]{1,0:T(8,128)(2,1)}) custom-call(s32[16]{0:T(128)S(1)} %dynamic-slice_bitcast_fusion.order_ref, bf16[672,512]{1,0:T(8,128)(2,1)S(1)} %slice_bitcast_fusion.refs_0_, bf16[608,512]{1,0:T(8,128)(2,1)S(1)} %slice_bitcast_fusion.1.refs_1_, bf16[672,512]{1,0:T(8,128)(2,1)S(1)} %collective-permute-done.refs_2_, ...), custom_call_target="tpu_custom_call" | custom-call | tf_op jit(solution)/shard_map/project/pallas_call | solution.py:219
  (111 shorter events, 29.0 us)
Async XLA Ops:
  12.4 271.4 %all-to-all-start = ((bf16[128,64,768]{2,1,0:T(8,128)(2,1)}), bf16[128,64,768]{2,1,0:T(8,128)(2,1)}, u32[]{:S(2)}, u32[]{:S(2)}) async-start(bf16[128,64,768]{2,1,0:T(8,128)(2,1)} %bitcast.10), calls=%async_computation | async-start | bytes 25165824 | tf_op jit(solution)/shard_map/all_to_all | solution.py:239
  23.6 164.4 %collective-permute-start.11 = (bf16[608,512]{1,0:T(8,128)(2,1)S(1)}, bf16[608,512]{1,0:T(8,128)(2,1)S(1)}, u32[]{:S(2)}, u32[]{:S(2)}) collective-permute-start(bf16[608,512]{1,0:T(8,128)(2,1)S(1)} %slice_bitcast_fusion.1.refs_1_), channel_id=1, source_target_pairs={{0,12},{4,0},{8,4},{12,8},{1,13},{5,1},{9,5},{13,9},{2,14},{6,2},{... | collective-permute-start | bytes 1867784 | tf_op jit(solution)/shard_map/ppermute | solution.py:73
  24.0 164.0 %collective-permute-start.7 = (bf16[608,512]{1,0:T(8,128)(2,1)S(1)}, bf16[608,512]{1,0:T(8,128)(2,1)S(1)}, u32[]{:S(2)}, u32[]{:S(2)}) collective-permute-start(bf16[608,512]{1,0:T(8,128)(2,1)S(1)} %slice_bitcast_fusion.1.refs_1_), channel_id=1, source_target_pairs={{0,4},{4,8},{8,12},{12,0},{1,5},{5,9},{9,13},{13,1},{2,6},{6,10},{... | collective-permute-start | bytes 1867784 | tf_op jit(solution)/shard_map/ppermute | solution.py:73
  25.1 164.5 %collective-permute-start.3 = (bf16[608,512]{1,0:T(8,128)(2,1)S(1)}, bf16[608,512]{1,0:T(8,128)(2,1)S(1)}, u32[]{:S(2)}, u32[]{:S(2)}) collective-permute-start(bf16[608,512]{1,0:T(8,128)(2,1)S(1)} %slice_bitcast_fusion.1.refs_1_), channel_id=1, source_target_pairs={{0,2},{2,0},{1,3},{3,1},{4,6},{6,4},{5,7},{7,5},{8,10},{10,8},{9,1... | collective-permute-start | bytes 1867784 | tf_op jit(solution)/shard_map/ppermute | solution.py:73
  26.5 176.2 %collective-permute-start.10 = (bf16[672,512]{1,0:T(8,128)(2,1)S(1)}, bf16[672,512]{1,0:T(8,128)(2,1)S(1)}, u32[]{:S(2)}, u32[]{:S(2)}) collective-permute-start(bf16[672,512]{1,0:T(8,128)(2,1)S(1)} %slice_bitcast_fusion.refs_0_), channel_id=1, source_target_pairs={{0,12},{4,0},{8,4},{12,8},{1,13},{5,1},{9,5},{13,9},{2,14},{6,2},{... | collective-permute-start | bytes 2064392 | tf_op jit(solution)/shard_map/ppermute | solution.py:73
  26.9 164.6 %collective-permute-start.1 = (bf16[608,512]{1,0:T(8,128)(2,1)S(1)}, bf16[608,512]{1,0:T(8,128)(2,1)S(1)}, u32[]{:S(2)}, u32[]{:S(2)}) collective-permute-start(bf16[608,512]{1,0:T(8,128)(2,1)S(1)} %slice_bitcast_fusion.1.refs_1_), channel_id=1, source_target_pairs={{0,1},{1,0},{2,3},{3,2},{4,5},{5,4},{6,7},{7,6},{8,9},{9,8},{10,11... | collective-permute-start | bytes 1867784 | tf_op jit(solution)/shard_map/ppermute | solution.py:100
  188.0 16.4 %collective-permute-start.6 = (bf16[672,512]{1,0:T(8,128)(2,1)S(1)}, bf16[672,512]{1,0:T(8,128)(2,1)S(1)}, u32[]{:S(2)}, u32[]{:S(2)}) collective-permute-start(bf16[672,512]{1,0:T(8,128)(2,1)S(1)} %slice_bitcast_fusion.refs_0_), channel_id=1, source_target_pairs={{0,4},{4,8},{8,12},{12,0},{1,5},{5,9},{9,13},{13,1},{2,6},{6,10},{... | collective-permute-start | bytes 2064392 | tf_op jit(solution)/shard_map/ppermute | solution.py:73
  188.0 18.2 %collective-permute-start.2 = (bf16[672,512]{1,0:T(8,128)(2,1)S(1)}, bf16[672,512]{1,0:T(8,128)(2,1)S(1)}, u32[]{:S(2)}, u32[]{:S(2)}) collective-permute-start(bf16[672,512]{1,0:T(8,128)(2,1)S(1)} %slice_bitcast_fusion.refs_0_), channel_id=1, source_target_pairs={{0,2},{2,0},{1,3},{3,1},{4,6},{6,4},{5,7},{7,5},{8,10},{10,8},{9,1... | collective-permute-start | bytes 2064392 | tf_op jit(solution)/shard_map/ppermute | solution.py:73
  189.7 17.8 %collective-permute-start = (bf16[672,512]{1,0:T(8,128)(2,1)S(1)}, bf16[672,512]{1,0:T(8,128)(2,1)S(1)}, u32[]{:S(2)}, u32[]{:S(2)}) collective-permute-start(bf16[672,512]{1,0:T(8,128)(2,1)S(1)} %slice_bitcast_fusion.refs_0_), channel_id=1, source_target_pairs={{0,1},{1,0},{2,3},{3,2},{4,5},{5,4},{6,7},{7,6},{8,9},{9,8},{10,11... | collective-permute-start | bytes 2064392 | tf_op jit(solution)/shard_map/ppermute | solution.py:100
  192.3 23.7 %collective-permute-start.23 = (bf16[608,512]{1,0:T(8,128)(2,1)S(1)}, bf16[608,512]{1,0:T(8,128)(2,1)S(1)}, u32[]{:S(2)}, u32[]{:S(2)}) collective-permute-start(bf16[608,512]{1,0:T(8,128)(2,1)S(1)} %collective-permute-done.11.refs_13_), channel_id=1, source_target_pairs={{0,12},{4,0},{8,4},{12,8},{1,13},{5,1},{9,5},{13,9},{2,14},{6,2},{... | collective-permute-start | bytes 1867784 | tf_op jit(solution)/shard_map/ppermute | solution.py:73
  202.7 15.1 %collective-permute-start.19 = (bf16[608,512]{1,0:T(8,128)(2,1)S(1)}, bf16[608,512]{1,0:T(8,128)(2,1)S(1)}, u32[]{:S(2)}, u32[]{:S(2)}) collective-permute-start(bf16[608,512]{1,0:T(8,128)(2,1)S(1)} %collective-permute-done.11.refs_13_), channel_id=1, source_target_pairs={{0,2},{2,0},{1,3},{3,1},{4,6},{6,4},{5,7},{7,5},{8,10},{10,8},{9,1... | collective-permute-start | bytes 1867784 | tf_op jit(solution)/shard_map/ppermute | solution.py:73
  204.3 13.9 %collective-permute-start.13 = (bf16[608,512]{1,0:T(8,128)(2,1)S(1)}, bf16[608,512]{1,0:T(8,128)(2,1)S(1)}, u32[]{:S(2)}, u32[]{:S(2)}) collective-permute-start(bf16[608,512]{1,0:T(8,128)(2,1)S(1)} %collective-permute-done.11.refs_13_), channel_id=1, source_target_pairs={{0,1},{1,0},{2,3},{3,2},{4,5},{5,4},{6,7},{7,6},{8,9},{9,8},{10,11... | collective-permute-start | bytes 1867784 | tf_op jit(solution)/shard_map/ppermute | solution.py:100
  206.1 24.5 %collective-permute-start.15 = (bf16[608,512]{1,0:T(8,128)(2,1)S(1)}, bf16[608,512]{1,0:T(8,128)(2,1)S(1)}, u32[]{:S(2)}, u32[]{:S(2)}) collective-permute-start(bf16[608,512]{1,0:T(8,128)(2,1)S(1)} %collective-permute-done.7.refs_9_), channel_id=1, source_target_pairs={{0,2},{2,0},{1,3},{3,1},{4,6},{6,4},{5,7},{7,5},{8,10},{10,8},{9,1... | collective-permute-start | bytes 1867784 | tf_op jit(solution)/shard_map/ppermute | solution.py:73
  207.4 23.3 %collective-permute-start.9 = (bf16[608,512]{1,0:T(8,128)(2,1)S(1)}, bf16[608,512]{1,0:T(8,128)(2,1)S(1)}, u32[]{:S(2)}, u32[]{:S(2)}) collective-permute-start(bf16[608,512]{1,0:T(8,128)(2,1)S(1)} %collective-permute-done.7.refs_9_), channel_id=1, source_target_pairs={{0,1},{1,0},{2,3},{3,2},{4,5},{5,4},{6,7},{7,6},{8,9},{9,8},{10,11... | collective-permute-start | bytes 1867784 | tf_op jit(solution)/shard_map/ppermute | solution.py:100
  216.0 17.5 %collective-permute-start.5 = (bf16[608,512]{1,0:T(8,128)(2,1)S(1)}, bf16[608,512]{1,0:T(8,128)(2,1)S(1)}, u32[]{:S(2)}, u32[]{:S(2)}) collective-permute-start(bf16[608,512]{1,0:T(8,128)(2,1)S(1)} %collective-permute-done.3.refs_5_), channel_id=1, source_target_pairs={{0,1},{1,0},{2,3},{3,2},{4,5},{5,4},{6,7},{7,6},{8,9},{9,8},{10,11... | collective-permute-start | bytes 1867784 | tf_op jit(solution)/shard_map/ppermute | solution.py:100
  217.8 16.6 %collective-permute-start.18 = (bf16[672,512]{1,0:T(8,128)(2,1)S(1)}, bf16[672,512]{1,0:T(8,128)(2,1)}, u32[]{:S(2)}, u32[]{:S(2)}) collective-permute-start(bf16[672,512]{1,0:T(8,128)(2,1)S(1)} %collective-permute-done.2.refs_4_), channel_id=1, source_target_pairs={{0,12},{4,0},{8,4},{12,8},{1,13},{5,1},{9,5},{13,9},{2,14},{6,2},{... | collective-permute-start | bytes 2064392 | tf_op jit(solution)/shard_map/ppermute | solution.py:73
  219.1 17.8 %collective-permute-start.12 = (bf16[672,512]{1,0:T(8,128)(2,1)S(1)}, bf16[672,512]{1,0:T(8,128)(2,1)S(1)}, u32[]{:S(2)}, u32[]{:S(2)}) collective-permute-start(bf16[672,512]{1,0:T(8,128)(2,1)S(1)} %collective-permute-done.10.refs_12_), channel_id=1, source_target_pairs={{0,1},{1,0},{2,3},{3,2},{4,5},{5,4},{6,7},{7,6},{8,9},{9,8},{10,11... | collective-permute-start | bytes 2064392 | tf_op jit(solution)/shard_map/ppermute | solution.py:100
  230.7 15.0 %collective-permute-start.22 = (bf16[672,512]{1,0:T(8,128)(2,1)S(1)}, bf16[672,512]{1,0:T(8,128)(2,1)}, u32[]{:S(2)}, u32[]{:S(2)}) collective-permute-start(bf16[672,512]{1,0:T(8,128)(2,1)S(1)} %collective-permute-done.6.refs_8_), channel_id=1, source_target_pairs={{0,4},{4,8},{8,12},{12,0},{1,5},{5,9},{9,13},{13,1},{2,6},{6,10},{... | collective-permute-start | bytes 2064392 | tf_op jit(solution)/shard_map/ppermute | solution.py:73
  231.5 15.4 %collective-permute-start.8 = (bf16[672,512]{1,0:T(8,128)(2,1)S(1)}, bf16[672,512]{1,0:T(8,128)(2,1)S(1)}, u32[]{:S(2)}, u32[]{:S(2)}) collective-permute-start(bf16[672,512]{1,0:T(8,128)(2,1)S(1)} %collective-permute-done.6.refs_8_), channel_id=1, source_target_pairs={{0,1},{1,0},{2,3},{3,2},{4,5},{5,4},{6,7},{7,6},{8,9},{9,8},{10,11... | collective-permute-start | bytes 2064392 | tf_op jit(solution)/shard_map/ppermute | solution.py:100
  234.4 26.0 %collective-permute-start.14 = (bf16[672,512]{1,0:T(8,128)(2,1)S(1)}, bf16[672,512]{1,0:T(8,128)(2,1)}, u32[]{:S(2)}, u32[]{:S(2)}) collective-permute-start(bf16[672,512]{1,0:T(8,128)(2,1)S(1)} %collective-permute-done.2.refs_4_), channel_id=1, source_target_pairs={{0,4},{4,8},{8,12},{12,0},{1,5},{5,9},{9,13},{13,1},{2,6},{6,10},{... | collective-permute-start | bytes 2064392 | tf_op jit(solution)/shard_map/ppermute | solution.py:73
  234.4 29.8 %collective-permute-start.4 = (bf16[672,512]{1,0:T(8,128)(2,1)S(1)}, bf16[672,512]{1,0:T(8,128)(2,1)S(1)}, u32[]{:S(2)}, u32[]{:S(2)}) collective-permute-start(bf16[672,512]{1,0:T(8,128)(2,1)S(1)} %collective-permute-done.2.refs_4_), channel_id=1, source_target_pairs={{0,1},{1,0},{2,3},{3,2},{4,5},{5,4},{6,7},{7,6},{8,9},{9,8},{10,11... | collective-permute-start | bytes 2064392 | tf_op jit(solution)/shard_map/ppermute | solution.py:100
  236.8 29.2 %collective-permute-start.27 = (bf16[336,512]{1,0:T(8,128)(2,1)S(1)}, bf16[336,512]{1,0:T(8,128)(2,1)S(1)}, u32[]{:S(2)}, u32[]{:S(2)}) collective-permute-start(bf16[336,512]{1,0:T(8,128)(2,1)S(1)} %slice.25), channel_id=1, source_target_pairs={{0,12},{4,0},{8,4},{12,8},{1,13},{5,1},{9,5},{13,9},{2,14},{6,2},{... | collective-permute-start | bytes 1032200 | tf_op jit(solution)/shard_map/ppermute | solution.py:73
  245.7 31.0 %collective-permute-start.28 = (bf16[608,512]{1,0:T(8,128)(2,1)S(1)}, bf16[608,512]{1,0:T(8,128)(2,1)}, u32[]{:S(2)}, u32[]{:S(2)}) collective-permute-start(bf16[608,512]{1,0:T(8,128)(2,1)S(1)} %collective-permute-done.23.refs_25_), channel_id=1, source_target_pairs={{0,2},{2,0},{1,3},{3,1},{4,6},{6,4},{5,7},{7,5},{8,10},{10,8},{9,1... | collective-permute-start | bytes 1867784 | tf_op jit(solution)/shard_map/ppermute | solution.py:73
  246.9 30.6 %collective-permute-start.25 = (bf16[608,512]{1,0:T(8,128)(2,1)S(1)}, bf16[608,512]{1,0:T(8,128)(2,1)S(1)}, u32[]{:S(2)}, u32[]{:S(2)}) collective-permute-start(bf16[608,512]{1,0:T(8,128)(2,1)S(1)} %collective-permute-done.23.refs_25_), channel_id=1, source_target_pairs={{0,1},{1,0},{2,3},{3,2},{4,5},{5,4},{6,7},{7,6},{8,9},{9,8},{10,11... | collective-permute-start | bytes 1867784 | tf_op jit(solution)/shard_map/ppermute | solution.py:100
  260.5 18.3 %collective-permute-start.21 = (bf16[608,512]{1,0:T(8,128)(2,1)S(1)}, bf16[608,512]{1,0:T(8,128)(2,1)S(1)}, u32[]{:S(2)}, u32[]{:S(2)}) collective-permute-start(bf16[608,512]{1,0:T(8,128)(2,1)S(1)} %collective-permute-done.19.refs_21_), channel_id=1, source_target_pairs={{0,1},{1,0},{2,3},{3,2},{4,5},{5,4},{6,7},{7,6},{8,9},{9,8},{10,11... | collective-permute-start | bytes 1867784 | tf_op jit(solution)/shard_map/ppermute | solution.py:100
  264.2 15.5 %collective-permute-start.17 = (bf16[608,512]{1,0:T(8,128)(2,1)S(1)}, bf16[608,512]{1,0:T(8,128)(2,1)S(1)}, u32[]{:S(2)}, u32[]{:S(2)}) collective-permute-start(bf16[608,512]{1,0:T(8,128)(2,1)S(1)} %collective-permute-done.15.refs_17_), channel_id=1, source_target_pairs={{0,1},{1,0},{2,3},{3,2},{4,5},{5,4},{6,7},{7,6},{8,9},{9,8},{10,11... | collective-permute-start | bytes 1867784 | tf_op jit(solution)/shard_map/ppermute | solution.py:100
  266.1 9.3 %collective-permute-start.26 = (bf16[336,512]{1,0:T(8,128)(2,1)S(1)}, bf16[336,512]{1,0:T(8,128)(2,1)}, u32[]{:S(2)}, u32[]{:S(2)}) collective-permute-start(bf16[336,512]{1,0:T(8,128)(2,1)S(1)} %slice.24), channel_id=1, source_target_pairs={{0,4},{4,8},{8,12},{12,0},{1,5},{5,9},{9,13},{13,1},{2,6},{6,10},{... | collective-permute-start | bytes 1032200 | tf_op jit(solution)/shard_map/ppermute | solution.py:73
  275.4 8.4 %collective-permute-start.20 = (bf16[672,512]{1,0:T(8,128)(2,1)}, bf16[672,512]{1,0:T(8,128)(2,1)}, u32[]{:S(2)}, u32[]{:S(2)}) collective-permute-start(bf16[672,512]{1,0:T(8,128)(2,1)} %collective-permute-done.18.refs_20_), channel_id=1, source_target_pairs={{0,1},{1,0},{2,3},{3,2},{4,5},{5,4},{6,7},{7,6},{8,9},{9,8},{10,11... | collective-permute-start | bytes 2064392 | tf_op jit(solution)/shard_map/ppermute | solution.py:100
  276.7 4.3 %collective-permute-start.30 = (bf16[336,512]{1,0:T(8,128)(2,1)S(1)}, bf16[336,512]{1,0:T(8,128)(2,1)S(1)}, u32[]{:S(2)}, u32[]{:S(2)}) collective-permute-start(bf16[336,512]{1,0:T(8,128)(2,1)S(1)} %collective-permute-done.27.refs_29_), channel_id=1, source_target_pairs={{0,1},{1,0},{2,3},{3,2},{4,5},{5,4},{6,7},{7,6},{8,9},{9,8},{10,11... | collective-permute-start | bytes 1032200 | tf_op jit(solution)/shard_map/ppermute | solution.py:100
  278.3 5.5 %collective-permute-start.24 = (bf16[672,512]{1,0:T(8,128)(2,1)}, bf16[672,512]{1,0:T(8,128)(2,1)}, u32[]{:S(2)}, u32[]{:S(2)}) collective-permute-start(bf16[672,512]{1,0:T(8,128)(2,1)} %collective-permute-done.22.refs_24_), channel_id=1, source_target_pairs={{0,1},{1,0},{2,3},{3,2},{4,5},{5,4},{6,7},{7,6},{8,9},{9,8},{10,11... | collective-permute-start | bytes 2064392 | tf_op jit(solution)/shard_map/ppermute | solution.py:100
  279.7 4.1 %collective-permute-start.16 = (bf16[672,512]{1,0:T(8,128)(2,1)}, bf16[672,512]{1,0:T(8,128)(2,1)}, u32[]{:S(2)}, u32[]{:S(2)}) collective-permute-start(bf16[672,512]{1,0:T(8,128)(2,1)} %collective-permute-done.14.refs_16_), channel_id=1, source_target_pairs={{0,1},{1,0},{2,3},{3,2},{4,5},{5,4},{6,7},{7,6},{8,9},{9,8},{10,11... | collective-permute-start | bytes 2064392 | tf_op jit(solution)/shard_map/ppermute | solution.py:100
  280.5 3.3 %collective-permute-start.31 = (bf16[608,512]{1,0:T(8,128)(2,1)}, bf16[608,512]{1,0:T(8,128)(2,1)}, u32[]{:S(2)}, u32[]{:S(2)}) collective-permute-start(bf16[608,512]{1,0:T(8,128)(2,1)} %collective-permute-done.28.refs_30_), channel_id=1, source_target_pairs={{0,1},{1,0},{2,3},{3,2},{4,5},{5,4},{6,7},{7,6},{8,9},{9,8},{10,11... | collective-permute-start | bytes 1867784 | tf_op jit(solution)/shard_map/ppermute | solution.py:100
  (36 other events, 270.5 us)
